TPU v7x, 256 devices: a whole 4x4x8 slice. The times are simulated.
256 devices in a mesh: seq: 32 (over y, z), grp: 8 (over x, core).
Axes of the slice: x: 4, y: 4, z: 8, core: 2. Of those that a mesh axis runs over, the one named last changes fastest.
Arguments:
- tokens: bfloat16 [16384, 2560], P('seq'), may hold values from -6 to 6
- norm_gain: float32 [2560], replicated, may hold values from 0.25 to 1.75
- inner_weight: bfloat16 [2560, 2, 5120], P(None, None, ('grp', 'seq')), may hold values from -0.125 to 0.125
- state_weight: bfloat16 [2560, 2, 128], replicated, may hold values from -0.125 to 0.125
- step_weight: bfloat16 [2560, 80], P(None, 'grp'), may hold values from -0.125 to 0.125
- step_bias: float32 [80], P('grp'), may hold values from -1 to 1
- decay_rate: float32 [80], P('grp'), may hold values from 1.2207031e-06 to 0.05
- skip_scale: float32 [80], P('grp'), may hold values from 0.5 to 1.5
- conv_inner: bfloat16 [4, 5120], P(None, 'grp'), may hold values from -3 to 3
- conv_state: bfloat16 [4, 2, 128], replicated, may hold values from -3 to 3
- out_gain: float32 [5120], P('grp'), may hold values from 0.25 to 1.75
- out_weight: bfloat16 [5120, 2560], P(None, 'grp'), may hold values from -0.078125 to 0.078125
Outputs:
- mixed: bfloat16 [16384, 2560], P('seq', 'grp')
All inputs are finite; a program needn't handle non-finite values.
Results may differ from a plain program's by a relative error of at most 0.0075.
Values may be sent and summed in bfloat16 or wider, within the bound.
A program may use at most 64 MiB of HBM per device.

v0:
```python
from functools import partial

import jax
import jax.numpy as jnp
from jax import lax
from jax.sharding import Mesh
from jax.sharding import PartitionSpec as P

SPAN = 256
SEQ = ("seq_0", "seq_1")
GRP_SEQ = ("grp", "seq_0", "seq_1")


EPS = 1e-05


def from_everyone(value, axis):
    copies = jnp.broadcast_to(value, (lax.axis_size(axis), *value.shape))
    return lax.all_to_all(copies, axis, split_axis=0, concat_axis=0, tiled=True)


def joined_along(pieces, dim):
    shape = list(pieces.shape[1:])
    shape[dim] *= pieces.shape[0]
    return jnp.moveaxis(pieces, 0, dim).reshape(shape)


def collect(value, axis, dim):
    pieces = from_everyone(value, axis)
    return joined_along(pieces, dim)


def from_behind(value, axis, steps):
    count = lax.axis_size(axis)
    leading, last = (max(0, -steps), min(count, count - steps))
    return lax.ppermute(value, axis, [(source, source + steps) for source in range(leading, last)])


def filled_with(value, identity):
    return jax.tree.map(
        lambda a, e: jnp.broadcast_to(jnp.asarray(e, a.dtype), a.shape), value, identity
    )


def carried_in(value, axes, combine, identity):
    before = start = filled_with(value, identity)
    total = value
    for axis in reversed(axes):
        length, place = (lax.axis_size(axis), lax.axis_index(axis))
        pieces = jax.tree.map(lambda part: lax.all_gather(part, axis), total)
        inside, total = (start, start)
        for k in range(length):
            passed = k < place
            total = combine(total, jax.tree.map(lambda part: part[k], pieces))
            inside = jax.tree.map(lambda new, old: jnp.where(passed, new, old), total, inside)
        before = combine(inside, before)
    return before


def conv_rows(before, current, weight):
    width = weight.shape[0]
    padded = jnp.concatenate([before, current], axis=0).astype(jnp.float32)
    length = current.shape[0]
    total = jnp.zeros(current.shape, jnp.float32)
    for offset in range(width):
        total = total + weight[offset].astype(jnp.float32) * padded[offset : offset + length]
    return jax.nn.silu(total).astype(jnp.bfloat16)


def span_step(rate, skip, state, inputs):
    xvals, bmat, cmat, delta = inputs
    logdec = -delta * rate[None, :]
    cumul = jnp.cumsum(logdec, axis=0)
    length = cumul.shape[0]
    scores = jnp.einsum("tn,sn->ts", cmat, bmat, preferred_element_type=jnp.float32)
    lower = jnp.arange(length)[:, None] >= jnp.arange(length)[None, :]
    diffs = cumul.T[:, :, None] - cumul.T[:, None, :]
    decay = jnp.exp(jnp.where(lower[None], diffs, -jnp.inf))
    mixer = (scores[None] * decay * delta.T[:, None, :]).astype(jnp.bfloat16)
    intra = jnp.einsum("hts,shp->thp", mixer, xvals, preferred_element_type=jnp.float32)
    inter = jnp.exp(cumul)[:, :, None] * jnp.einsum("tn,hpn->thp", cmat.astype(jnp.float32), state)
    output = intra + inter + skip[None, :, None] * xvals.astype(jnp.float32)
    tail = jnp.exp(cumul[-1][None, :] - cumul) * delta
    weighted = (tail[:, :, None] * bmat.astype(jnp.float32)[:, None, :]).astype(jnp.bfloat16)
    update = jnp.einsum("shp,shn->hpn", xvals, weighted, preferred_element_type=jnp.float32)
    new_state = jnp.exp(cumul[-1])[:, None, None] * state + update
    return (new_state, output)


def body(
    tokens,
    norm_gain,
    inner_weight,
    state_weight,
    step_weight,
    step_bias,
    decay_rate,
    skip_scale,
    conv_inner,
    conv_state,
    out_gain,
    out_weight,
):
    tok_rows = tokens.shape[0]
    model_width = tokens.shape[1]
    wide = tokens.astype(jnp.float32)
    normed = (
        wide * lax.rsqrt(jnp.mean(wide * wide, axis=1, keepdims=True) + EPS) * norm_gain
    ).astype(jnp.bfloat16)
    piece = lax.all_gather(inner_weight, SEQ, axis=2, tiled=True)
    count = piece.shape[2]
    flat = piece.reshape(piece.shape[0], 2 * count)
    result = jnp.dot(normed, flat, preferred_element_type=jnp.float32).astype(jnp.bfloat16)
    inner = result.reshape(tok_rows, 2, count)
    state_flat = state_weight.reshape(model_width, -1)
    share = tok_rows // lax.axis_size("grp")
    begin = lax.axis_index("grp") * share
    own_rows = lax.dynamic_slice_in_dim(normed, begin, share, 0)
    made = jnp.dot(own_rows, state_flat, preferred_element_type=jnp.float32).astype(jnp.bfloat16)
    state_pre = collect(made, "grp", 0).reshape(tok_rows, 2, -1)
    delta = jax.nn.softplus(
        jnp.dot(normed, step_weight, preferred_element_type=jnp.float32) + step_bias
    )
    inner_values = inner[:, 0, :]
    width = conv_inner.shape[0]
    first_kept = tok_rows - width + 1
    before_values, before_state = from_behind(
        (inner_values[first_kept:], state_pre[first_kept:]), SEQ, 1
    )
    values = conv_rows(before_values, inner_values, conv_inner)
    conv_out = conv_rows(before_state, state_pre, conv_state)
    heads_here = delta.shape[1]
    head_width = values.shape[1] // heads_here
    state_width = conv_out.shape[2]
    blocks = tok_rows // SPAN
    xs_blocks = values.reshape(blocks, SPAN, heads_here, head_width)
    b_blocks = conv_out[:, 0, :].reshape(blocks, SPAN, state_width)
    c_blocks = conv_out[:, 1, :].reshape(blocks, SPAN, state_width)
    d_blocks = delta.reshape(blocks, SPAN, heads_here)
    initial = jnp.zeros((heads_here, head_width, state_width), jnp.float32)
    final_state, outputs = lax.scan(
        partial(span_step, decay_rate, skip_scale),
        initial,
        (xs_blocks, b_blocks, c_blocks, d_blocks),
    )
    cumdev = jnp.cumsum(-delta * decay_rate[None, :], axis=0)
    totals = cumdev[-1]

    def combine(earlier, later):
        return (earlier[0] + later[0], jnp.exp(later[0])[:, None, None] * earlier[1] + later[1])

    scanned = carried_in(
        (totals, final_state), SEQ, combine, (jnp.zeros_like(totals), jnp.zeros_like(final_state))
    )
    incoming = scanned[1]
    cmat_wide = conv_out[:, 1, :].astype(jnp.float32)
    carried = jnp.exp(cumdev)[:, :, None] * jnp.einsum("tn,hpn->thp", cmat_wide, incoming)
    mixed_heads = (outputs.reshape(tok_rows, heads_here, head_width) + carried).reshape(
        tok_rows, heads_here * head_width
    )
    gated = mixed_heads * jax.nn.silu(inner[:, 1, :].astype(jnp.float32))
    squares = lax.psum(jnp.sum(gated * gated, axis=1), "grp")
    row_scale = lax.rsqrt(squares / (lax.axis_size("grp") * gated.shape[1]) + EPS)
    scaled = (gated * out_gain).astype(jnp.bfloat16)
    regrouped = lax.all_to_all(out_weight, "grp", split_axis=0, concat_axis=1, tiled=True)
    partial_sums = jnp.dot(scaled, regrouped, preferred_element_type=jnp.float32)
    summed = lax.psum_scatter(partial_sums, "grp", scatter_dimension=1, tiled=True)
    return (summed * row_scale[:, None]).astype(jnp.bfloat16)


def solution(mesh):
    finer = Mesh(mesh.devices.reshape(4, 8, mesh.shape["grp"]), ("seq_0", "seq_1", "grp"))
    return jax.shard_map(
        body,
        mesh=finer,
        in_specs=(
            P(SEQ, None),
            P(),
            P(None, None, GRP_SEQ),
            P(),
            P(None, "grp"),
            P("grp"),
            P("grp"),
            P("grp"),
            P(None, "grp"),
            P(),
            P("grp"),
            P(None, "grp"),
        ),
        out_specs=P(SEQ, "grp"),
        check_vma=False,
    )
```

profile of v0, /device:TPU:1, one launch (start us, length us, event | category | flops | bytes accessed | tf_op | source)
XLA Modules:
  0.0 286.9 jit_solution(9522031187306692972)
XLA Ops:
  7.3 2.5 fusion.37
  12.2 6.5 %all-to-all-start = ((bf16[8,64,256]{2,1,0:T(8,128)(2,1)}), bf16[8,64,256]{2,1,0:T(8,128)(2,1)S(1)}, u32[]{:S(2)}, u32[]{:S(2)}) async-start(bf16[8,64,256]{2,1,0:T(8,128)(2,1)} %broadcast_in_dim.16), calls=%async_computation | async-start | bytes 524288 | tf_op jit(solution)/shard_map/all_to_all | solution.py:19
  18.8 0.8 compare_select_fusion.1
  19.6 5.6 %all-to-all-done = bf16[8,64,256]{2,1,0:T(8,128)(2,1)S(1)} async-done(((bf16[8,64,256]{2,1,0:T(8,128)(2,1)}), bf16[8,64,256]{2,1,0:T(8,128)(2,1)S(1)}, u32[]{:S(2)}, u32[]{:S(2)}) %all-to-all-start) | async-done | bytes 262176 | tf_op jit(solution)/shard_map/all_to_all | solution.py:19
  25.3 2.8 collective-permute-start.1
  30.0 72.6 %all-gather.7.cloned.1.call-done = bf16[2560,2,640]{0,1,2:T(2,128)(2,1)} async-done(((bf16[2560,2,20]{0,1,2:T(2,128)(2,1)}), bf16[2560,2,640]{0,1,2:T(2,128)(2,1)}) %all-gather.7.cloned.1.call-update) | async-done | bytes 6553616 | tf_op jit(solution)/shard_map/all_gather | solution.py:110
  102.6 4.0 %copy.85 = bf16[2560,2,640]{0,2,1:T(8,128)(2,1)S(1)} copy(bf16[2560,2,640]{0,1,2:T(2,128)(2,1)} %all-gather.7.cloned.1.call-done) | data formatting | bytes 13107200 | tf_op jit(solution)/shard_map/all_gather | solution.py:110
  106.6 3.6 %convolution_convert_fusion = bf16[512,1280]{1,0:T(8,128)(2,1)S(1)} fusion(bf16[512,2560]{1,0:T(8,128)(2,1)S(1)} %copy-done.4, bf16[2560,1280]{0,1:T(8,128)(2,1)S(1)} %bitcast.324), kind=kOutput, calls=%fused_computation.56 | convolution fusion | flops 3356098560 | bytes 10485760 | tf_op jit(solution)/shard_map/dot_general | solution.py:113
  111.0 1.4 collective-permute-start
  112.4 0.9 fusion.131
  113.6 1.0 collective-permute-done
  116.6 36.3 %while.13 = (s32[]{:T(128)}, f32[10,64,128]{2,1,0:T(8,128)S(1)}, f32[2,256,10,64]{1,0,3,2:T(2,128)}, f32[2,256,10]{1,0,2:T(2,128)S(1)}, f32[10]{0:T(128)S(1)}, /...) while((s32[]{:T(128)}, f32[10,64,128]{2,1,0:T(8,128)S(1)}, ...), condition=%wide.region_4.5_spmd.clone, body=%wide.region_1.4_spmd.clone.sunk | while | flops 190064672 | bytes 8083440 | solution.py:141
  118.4 0.9 fusion.157
  120.6 14.1 %dynamic_update_slice.6 = f32[2,256,10,64]{1,0,3,2:T(2,128)} dynamic-update-slice(f32[2,256,10,64]{1,0,3,2:T(2,128)} %get-tuple-element.265, f32[1,256,10,64]{1,0,3,2:T(1,128)S(1)} %copy.142, s32[]{:T(128)S(6)} %copy.147, s32[]{:T(128)} %constant.28.clone.1..sunk, s32[]{:T(128)} %constant.28.clone.1..sunk, s32[]{:T(128)} %constant.28.clone.1..sunk) | dynamic-update-slice | bytes 1310724 | tf_op jit(solution)/shard_map/while/body/jit(dynamic_update_index_in_dim)/dynamic_update_slice | solution.py:141
  136.6 0.9 fusion.157
  138.8 14.1 %dynamic_update_slice.6 = f32[2,256,10,64]{1,0,3,2:T(2,128)} dynamic-update-slice(f32[2,256,10,64]{1,0,3,2:T(2,128)} %get-tuple-element.265, f32[1,256,10,64]{1,0,3,2:T(1,128)S(1)} %copy.142, s32[]{:T(128)S(6)} %copy.147, s32[]{:T(128)} %constant.28.clone.1..sunk, s32[]{:T(128)} %constant.28.clone.1..sunk, s32[]{:T(128)} %constant.28.clone.1..sunk) | dynamic-update-slice | bytes 1310724 | tf_op jit(solution)/shard_map/while/body/jit(dynamic_update_index_in_dim)/dynamic_update_slice | solution.py:141
  153.7 3.9 %copy.130 = bf16[40,8,8,640]{3,2,0,1:T(8,128)(2,1)} copy(bf16[40,8,8,640]{3,2,1,0:T(8,128)(2,1)} %bitcast.329) | data formatting | bytes 6553600 | tf_op jit(solution)/shard_map/all_to_all | solution.py:165
  157.6 7.9 %all-to-all-start.1 = ((bf16[8,640,320]{1,2,0:T(8,128)(2,1)}), bf16[8,640,320]{1,2,0:T(8,128)(2,1)S(1)}, u32[]{:S(2)}, u32[]{:S(2)}) async-start(bf16[8,640,320]{1,2,0:T(8,128)(2,1)} %bitcast.293), calls=%async_computation.1 | async-start | bytes 6553600 | tf_op jit(solution)/shard_map/all_to_all | solution.py:165
  165.6 1.2 reduce-window.16
  167.3 13.9 %all-gather.1 = f32[8,1,10]{2,1,0:T(1,128)S(1)} all-gather(f32[1,1,10]{2,1,0:T(1,128)S(1)} %bitcast.341), channel_id=1, replica_groups=mesh['seq_0'=4,'seq_1'=8,'grp'=8] {'seq_1'}, dimensions={0}, use_global_device_ids=true | all-gather | bytes 360 | tf_op jit(solution)/shard_map/all_gather | solution.py:50
  181.3 13.8 %all-gather.11.cloned.1.call-done = f32[80,64,128]{2,1,0:T(8,128)} async-done(((f32[10,64,128]{2,1,0:T(8,128)}), f32[80,64,128]{2,1,0:T(8,128)}) %all-gather.11.cloned.1.call-update) | async-done | bytes 2621456 | tf_op jit(solution)/shard_map/all_gather | solution.py:50
  195.1 2.7 fusion.59
  198.0 8.4 %all-gather.2 = f32[4,1,10]{2,1,0:T(1,128)S(1)} all-gather(f32[1,1,10]{2,1,0:T(1,128)S(1)} %get-tuple-element.173), channel_id=1, replica_groups=mesh['seq_0'=4,'seq_1'=8,'grp'=8] {'seq_0'}, dimensions={0}, use_global_device_ids=true | all-gather | bytes 200 | tf_op jit(solution)/shard_map/all_gather | solution.py:50
  206.4 2.2 copy.103
  208.6 2.4 copy.98
  211.0 3.3 %reshape.259 = f32[512,10,64]{0,2,1:T(8,128)} reshape(f32[2,256,10,64]{1,0,3,2:T(2,128)} %get-tuple-element.53) | data formatting | bytes 2621440 | tf_op jit(solution)/shard_map/reshape | solution.py:158
  214.3 12.1 %all-gather.9.cloned.1.call-done = f32[4,10,64,128]{3,2,1,0:T(8,128)} async-done(((f32[1,10,64,128]{3,2,1,0:T(8,128)}), f32[4,10,64,128]{3,2,1,0:T(8,128)}) %all-gather.9.cloned.1.call-update) | async-done | bytes 1310736 | tf_op jit(solution)/shard_map/all_gather | solution.py:50
  226.4 4.7 %multiply_reduce_fusion = (f32[512]{0:T(512)S(1)}, bf16[512,10,64]{0,2,1:T(8,128)(2,1)}) fusion(f32[10,64]{1,0:T(8,128)S(1)} %mul.452, f32[512,10,64]{0,2,1:T(8,128)} %bitcast.336, f32[512,10,64]{0,2,1:T(8,128)} %reshape.259, f32[4,10,64,128]{3,2,1,0:T(8,128)} %all-gather.9.cloned.1.call-done, f32[1,10,64,128]{3,2,1,0:T(8,128)} %get-tuple-element.163, ...), kind=kOutput, calls=%fused_computation.70 | convolution fusion | flops 90111488 | bytes 7365572 | tf_op jit(solution)/shard_map/tn,hpn->thp/dot_general | solution.py:157
  231.1 5.6 %fusion.133 = f32[512,2560]{0,1:T(8,128)} fusion(bf16[640,2560]{0,1:T(8,128)(2,1)S(1)} %bitcast.330, bf16[512,640]{0,1:T(8,128)(2,1)} %bitcast.343), kind=kOutput, calls=%fused_computation.216 | convolution fusion | flops 1677721600 | bytes 9175040 | tf_op jit(solution)/shard_map/dot_general | solution.py:166
  236.7 13.5 %psum.7 = f32[512]{0:T(512)S(1)} all-reduce(f32[512]{0:T(512)S(1)} %get-tuple-element.167), channel_id=1, replica_groups=mesh['seq_0'=4,'seq_1'=8,'grp'=8] {'grp'}, use_global_device_ids=true, to_apply=%region_9.10 | all-reduce | flops 512 | bytes 4096 | tf_op jit(solution)/shard_map/psum | solution.py:162
  250.3 28.3 %reduce-scatter.2.cloned.1.call-done = f32[512,320]{0,1:T(8,128)} async-done(((f32[512,2560]{0,1:T(8,128)}), f32[512,320]{0,1:T(8,128)}) %reduce-scatter.2.cloned.1.call-update) | async-done | bytes 655376 | tf_op jit(solution)/shard_map/reduce_scatter | solution.py:167
  278.5 1.9 multiply_convert_fusion.14
  (124 shorter events, 15.7 us)
Async XLA Ops:
  6.5 12.2 %copy-start = (bf16[2560,10]{0,1:T(8,128)(2,1)S(1)}, bf16[2560,10]{0,1:T(8,128)(2,1)}, u32[]{:S(2)}) copy-start(bf16[2560,10]{0,1:T(8,128)(2,1)} %param.18) | copy-start | bytes 153604
  6.5 96.0 %all-gather.7.cloned.1.call-start = ((), (), s32[]{:S(2)}) async-start(), calls=%async_computation.3 | async-start | bytes 6758400 | tf_op jit(solution)/shard_map/all_gather | solution.py:110
  6.5 3.2 %copy-start.8 = (f32[2560]{0:T(1024)S(1)}, f32[2560]{0:T(1024)}, u32[]{:S(2)}) copy-start(f32[2560]{0:T(1024)} %param.15) | copy-start | bytes 30724
  7.3 2.5 copy-start.2
  9.8 1.3 copy-start.12
  10.5 9.1 %copy-start.3 = (bf16[512,2560]{1,0:T(8,128)(2,1)}, bf16[512,2560]{1,0:T(8,128)(2,1)S(1)}, u32[]{:S(2)}) copy-start(bf16[512,2560]{1,0:T(8,128)(2,1)S(1)} %fusion.39) | copy-start | bytes 7864324
  10.5 8.3 %copy-start.11 = (f32[10]{0:T(128)S(1)}, f32[10]{0:T(128)}, u32[]{:S(2)}) copy-start(f32[10]{0:T(128)} %param.19) | copy-start | bytes 124
  12.2 13.0 %all-to-all-start = ((bf16[8,64,256]{2,1,0:T(8,128)(2,1)}), bf16[8,64,256]{2,1,0:T(8,128)(2,1)S(1)}, u32[]{:S(2)}, u32[]{:S(2)}) async-start(bf16[8,64,256]{2,1,0:T(8,128)(2,1)} %broadcast_in_dim.16), calls=%async_computation | async-start | bytes 524288 | tf_op jit(solution)/shard_map/all_to_all | solution.py:19
  18.7 0.9 copy-start.10
  18.7 9.4 %copy-start.6 = (bf16[4,640]{1,0:T(4,128)(2,1)S(1)}, bf16[4,640]{1,0:T(4,128)(2,1)}, u32[]{:S(2)}) copy-start(bf16[4,640]{1,0:T(4,128)(2,1)} %param.22) | copy-start | bytes 15364
  18.7 176.4 %all-gather.11.cloned.1.call-start = ((), (), s32[]{:S(2)}) async-start(), calls=%async_computation.6 | async-start | bytes 2949120 | tf_op jit(solution)/shard_map/all_gather | solution.py:50
  25.3 3.5 %collective-permute-start.1 = (bf16[3,2,128]{2,0,1:T(4,128)(2,1)S(1)}, bf16[3,2,128]{2,0,1:T(4,128)(2,1)S(1)}, u32[]{:S(2)}, u32[]{:S(2)}) collective-permute-start(bf16[3,2,128]{2,0,1:T(4,128)(2,1)S(1)} %slice.243), channel_id=1, source_target_pairs={{0,8},{8,16},{16,24},{24,32},{32,40},{40,48},{48,56},{56,64},{64,7... | collective-permute-start | bytes 4616 | tf_op jit(solution)/shard_map/ppermute | solution.py:36
  29.3 0.7 copy-start.5
  102.6 4.0 %copy-start.4 = (bf16[512,2560]{1,0:T(8,128)(2,1)S(1)}, bf16[512,2560]{1,0:T(8,128)(2,1)}, u32[]{:S(2)}) copy-start(bf16[512,2560]{1,0:T(8,128)(2,1)} %copy-done.3) | copy-start | bytes 7864324
  111.0 3.6 %collective-permute-start = (bf16[3,640]{0,1:T(8,128)(2,1)S(1)}, bf16[3,640]{0,1:T(8,128)(2,1)S(1)}, u32[]{:S(2)}, u32[]{:S(2)}) collective-permute-start(bf16[3,640]{0,1:T(8,128)(2,1)S(1)} %slice_bitcast_fusion.8), channel_id=1, source_target_pairs={{0,8},{8,16},{16,24},{24,32},{32,40},{40,48},{48,56},{56,64},{64,7... | collective-permute-start | bytes 11528 | tf_op jit(solution)/shard_map/ppermute | solution.py:36
  115.9 0.7 copy-start.7
  115.9 0.7 copy-start.13
  152.9 0.7 copy-start.1
  157.6 73.5 %all-to-all-start.1 = ((bf16[8,640,320]{1,2,0:T(8,128)(2,1)}), bf16[8,640,320]{1,2,0:T(8,128)(2,1)S(1)}, u32[]{:S(2)}, u32[]{:S(2)}) async-start(bf16[8,640,320]{1,2,0:T(8,128)(2,1)} %bitcast.293), calls=%async_computation.1 | async-start | bytes 6553600 | tf_op jit(solution)/shard_map/all_to_all | solution.py:165
  165.5 60.9 %all-gather.9.cloned.1.call-start = ((), (), s32[]{:S(2)}) async-start(), calls=%async_computation.4 | async-start | bytes 1638400 | tf_op jit(solution)/shard_map/all_gather | solution.py:50
  195.1 2.8 copy-start.9
  197.8 80.7 %reduce-scatter.2.cloned.1.call-start = ((), (), s32[]{:S(2)}) async-start(), calls=%async_computation.5 | async-start | bytes 5898240 | tf_op jit(solution)/shard_map/reduce_scatter | solution.py:167
Sparse Core Ops, SparseCore 0:
  9.9 92.6 all-gather.6
  153.8 41.2 all-gather.10
  198.0 28.3 all-gather.8
  236.8 41.6 reduce-scatter.1
where the time goes:
time: 291 us; the launch traced here: 287 us
  waiting for transfers between devices  135 us (46%)
  local copies, waits for them, and re-layouts  52.7 us (18%)
  blocking collectives  35.8 us (12%)
  matrix products  18.9 us (6%)
  starting transfers between devices  18.7 us (6%)
  between operations  13.5 us (5%)
  other arithmetic  12.3 us (4%)
    all_gather x1, waiting for transfers between devices, body(): piece = lax.all_gather(inner_weight, SEQ, axis=2, tiled=True)  72.6 us
    dynamic_update_slice x4, local copies, waits for them, and re-layouts, body(): lax.scan(partial(span_step, decay_rate, skip_scale), initial, (xs_blocks,...  29.6 us
    reduce_scatter x1, waiting for transfers between devices, body(): lax.psum_scatter(partial_sums, 'grp', scatter_dimension=1, tiled=True)  28.3 us
    all_gather x2, waiting for transfers between devices, carried_in(): pieces = jax.tree.map(lambda part: lax.all_gather(part, axis), total)  26 us
    all_gather x2, blocking collectives, carried_in(): pieces = jax.tree.map(lambda part: lax.all_gather(part, axis), total)  22.3 us
    psum x1, blocking collectives, body(): squares = lax.psum(jnp.sum(gated * gated, axis=1), 'grp')  13.5 us
    all_to_all x1, starting transfers between devices, body(): lax.all_to_all(out_weight, 'grp', split_axis=0, concat_axis=1, tiled=True)  7.94 us
    all_to_all x1, starting transfers between devices, from_everyone(): return lax.all_to_all(copies, axis, split_axis=0, concat_axis=0, tiled=True)  6.51 us
  transfers between devices with their start and end apart: 8, of which 7 were waited for; matrix products, arithmetic and copies ran while one was open for 10% of the time, Pallas kernels for 0%

commit v1 on v0

v1 whole, which is shorter than its diff:
```python
import functools

import jax
import jax.numpy as jnp
from jax import lax
from jax.experimental import pallas as pl
from jax.experimental.pallas import tpu as pltpu
from jax.sharding import PartitionSpec as P

MESH = pl.DeviceIdType.MESH
BF = jnp.bfloat16
F32 = jnp.float32
EPS = 1e-05

TOK = 512
D = 2560
CH = 640
HEADS = 10
SPAN = 256
KA, KB = 512, 768
FEAT = 320
NY, NZ, NX = 4, 8, 4


def dot(a, b):
    return jnp.dot(a, b, preferred_element_type=F32)


def half_messages(h):
    m = {}
    for d in (1, -1):
        m["Ay", h, d] = (("y", d), 0.88, [])
        m["Ay2", h, d] = (("y", d), 0.44, [("Ay", h, d)])
        for k in range(1, 5):
            rels = (0, -1, 1, 2) if k < 4 else ((0, -1) if d == 1 else (1, 2))
            for rel in rels:
                if k > 1:
                    dep = [("Az", h, d, k - 1, rel)]
                else:
                    dep = {
                        0: [],
                        -1: [("Ay", h, 1)],
                        1: [("Ay", h, -1)],
                        2: [("Ay2", h, 1), ("Ay2", h, -1)],
                    }[rel]
                m["Az", h, d, k, rel] = (("z", d), 0.88, dep)
            dep = [("Bz", h, d, k - 1)] if k > 1 else []
            m["Bz", h, d, k] = (("z", d), 1.32 if k < 4 else 0.66, dep)
        for zr in range(-3, 5):
            if zr == 0:
                dep = []
            elif zr == 4:
                dep = [("Bz", h, 1, 4), ("Bz", h, -1, 4)]
            else:
                dep = [("Bz", h, 1, -zr)] if zr < 0 else [("Bz", h, -1, zr)]
            m["By", h, d, zr] = (("y", d), 1.32, dep)
            if (zr <= 0) == (d == 1):
                m["By2", h, d, zr] = (("y", d), 1.32, [("By", h, d, zr)])
    return m


def build_schedule():
    msgs = {}
    for d in (1, -1):
        msgs["X2", d] = (("x", d), 10.5, [])
        msgs["X1", d] = (("x", d), 21.0, [])
        msgs["X2f", d] = (("x", d), 10.5, [("X2", d)])
    for h in (0, 1):
        msgs.update(half_messages(h))
    order = {k: i for i, k in enumerate(msgs)}

    def rank(k):
        h = k[1] if k[0][0] in "AB" else 0
        fan = 0 if k[0] in ("Bz", "Ay", "X2", "X2f") else 1
        return (h, fan, order[k])

    latency = 2.2
    arrived, started = {}, {}
    free = {}
    pending = set(msgs)
    while pending:
        best = None
        for k in pending:
            link, dur, deps = msgs[k]
            if any(q not in arrived for q in deps):
                continue
            ready = max([arrived[q] for q in deps], default=0.0)
            t = max(ready, free.get(link, 0.0))
            key = (t, rank(k))
            if best is None or key < best[0]:
                best = (key, k, t)
        _, k, t = best
        link, dur, _ = msgs[k]
        started[k] = t
        free[link] = t + dur
        arrived[k] = t + dur + latency
        pending.remove(k)
    events = []
    for k in msgs:
        ready = max([arrived[q] for q in msgs[k][2]], default=0.0)
        events.append((max(ready, started[k] - 3.0), started[k], order[k], k))
    events.sort()
    half_done = [max(arrived[k] for k in msgs if k[0][0] in "AB" and k[1] == h) for h in (0, 1)]
    return msgs, [(e[0], e[3]) for e in events], half_done


MSGS, EVENTS, HALF_DONE = build_schedule()
IDS = {k: i for i, k in enumerate(MSGS)}
N_MSG = len(MSGS)


def kernel(
    tok, gain, own_a, own_b, sw, st, bias, rate, skip, cwin, cwst, og, ow,
    out,
    wa, wb, nrm, nt, spf, cb, ct, dec, cum, ecum, tailw, d01, scores, mix, colt,
    p0s, p1s, inn, gat, vt, vw, u, yv, cs, cr, co, ci, tt, rowd, prefix,
    sbf, s_t, scb, wr, relay, sq, rs_out, rs_in1, rs2_out, rs2_in, own_p,
    halo, send, recv, xsend, xrecv, lsem,
):
    seq = lax.axis_index("seq")
    grp = lax.axis_index("grp")
    y, z = seq // NZ, lax.rem(seq, NZ)
    x, c = grp // 2, lax.rem(grp, 2)

    def yy(d):
        return lax.rem(y + d + NY, NY)

    def zz(d):
        return lax.rem(z + d + NZ, NZ)

    def xx(d):
        return lax.rem(x + d + NX, NX)

    def dev(dy=0, dz=0, dx=0, dc=0):
        return (yy(dy) * NZ + zz(dz), xx(dx) * 2 + lax.rem(c + dc, 2))

    nxt = (lax.rem(seq + 1, NY * NZ), grp)
    prv = (lax.rem(seq + NY * NZ - 1, NY * NZ), grp)

    barrier = pltpu.get_barrier_semaphore()
    peers = [nxt, prv]
    peers += [dev(dz=k) for k in range(1, NZ)]
    peers += [dev(dy=k) for k in range(1, NY)]
    peers += [dev(dx=k // 2, dc=k % 2) for k in range(1, 8)]
    for p in peers:
        pl.semaphore_signal(barrier, inc=1, device_id=p, device_id_type=MESH)

    own_out = pltpu.make_async_copy(
        ow.at[pl.ds(pl.multiple_of(x * 1280, 1280), 1280)], wr.at[x], lsem.at[0]
    )
    own_out.start()
    own_in = []
    for h in (0, 1):
        own_in.append(pltpu.make_async_copy(own_a.at[h], wa.at[h, y, z], lsem.at[1 + h]))
        own_in.append(pltpu.make_async_copy(own_b.at[h], wb.at[h, y, z], lsem.at[3 + h]))
    for q in own_in:
        q.start()
    nrm[0:128, :] = jnp.zeros((128, D), BF)
    pl.semaphore_wait(barrier, len(peers))

    def remote(src, dst, s, r, to):
        return pltpu.make_async_remote_copy(
            src_ref=src, dst_ref=dst, send_sem=s, recv_sem=r, device_id=to, device_id_type=MESH
        )

    def message(k):
        i = IDS[k]
        kind = k[0]
        if kind[0] == "X":
            d = k[1]
            if kind == "X1":
                src = ow.at[pl.ds(pl.multiple_of(xx(d) * 1280, 1280), 1280)]
                dst = wr.at[x]
            elif kind == "X2":
                off = 0 if d == 1 else 640
                src = ow.at[pl.ds(pl.multiple_of(xx(2) * 1280, 1280) + off, 640)]
                dst = relay.at[0 if d == 1 else 1]
            else:
                off = 0 if d == 1 else 640
                src = relay.at[0 if d == 1 else 1]
                dst = wr.at[xx(-d), pl.ds(off, 640)]
            return remote(src, dst, send.at[i], recv.at[i], dev(dx=d))
        h, d = k[1], k[2]
        if kind == "Ay":
            src, dst, to = own_a.at[h], wa.at[h, y, z], dev(dy=d)
        elif kind == "Ay2":
            cols = pl.ds(0 if d == 1 else KA // 2, KA // 2)
            src = dst = wa.at[h, yy(-d), z, :, cols]
            to = dev(dy=d)
        elif kind == "Az":
            step, rel = k[3], k[4]
            dst = wa.at[h, yy(rel), zz(-d * (step - 1))]
            src = own_a.at[h] if (step == 1 and rel == 0) else dst
            to = dev(dz=d)
        elif kind == "Bz":
            step = k[3]
            dst = wb.at[h, y, zz(-d * (step - 1))]
            src = own_b.at[h] if step == 1 else dst
            if step == 4:
                cols = pl.ds(0 if d == 1 else KB // 2, KB // 2)
                src = dst = wb.at[h, y, zz(-d * 3), :, cols]
            to = dev(dz=d)
        elif kind == "By":
            zr = k[3]
            dst = wb.at[h, y, zz(zr)]
            src = own_b.at[h] if zr == 0 else dst
            to = dev(dy=d)
        else:
            src = dst = wb.at[h, yy(-d), zz(k[3])]
            to = dev(dy=d)
        return remote(src, dst, send.at[i], recv.at[i], to)

    waited = set()
    queue = list(EVENTS)

    def take(k):
        if k not in waited:
            waited.add(k)
            message(k).wait_recv()

    def progress(until):
        while queue and queue[0][0] <= until:
            _, k = queue.pop(0)
            for q in MSGS[k][2]:
                take(q)
            message(k).start()

    def complete(h):
        for k in MSGS:
            if k[0][0] in "AB" and k[1] == h:
                take(k)

    extra_sends = []

    def extra(src, dst, to, slot):
        q = remote(src, dst, xsend.at[slot], xrecv.at[slot], to)
        q.start()
        extra_sends.append(q)
        return q

    halo_copy = extra(tok.at[pl.ds(TOK - 16, 16)], halo, nxt, 0)

    def norm_rows(v):
        wide = v.astype(F32)
        ms = jnp.mean(wide * wide, axis=1, keepdims=True)
        return wide * lax.rsqrt(ms + EPS) * gain[...]

    def piece_norm(part):
        def step(i, carry):
            r = pl.multiple_of(part * 128 + i * 16, 16)
            nrm[pl.ds(128 + r, 16), :] = norm_rows(tok[pl.ds(r, 16), :]).astype(BF)
            return carry

        lax.fori_loop(0, 8, step, 0)

    def piece_halo():
        halo_copy.wait_recv()
        n = jnp.where(seq > 0, norm_rows(halo[...]), 0.0)
        nrm[112:128, :] = n.astype(BF)

    def piece_transpose(tb):
        def step(i, carry):
            k = pl.multiple_of(i * 128, 128)
            nt[pl.ds(k, 128), tb * 128 : (tb + 1) * 128] = nrm[
                tb * 128 : (tb + 1) * 128, pl.ds(k, 128)
            ].T
            return carry

        lax.fori_loop(0, D // 128, step, 0)

    def piece_state(part):
        r = part * 176
        got = dot(nrm[112 + r : 112 + r + 176, :], sw[...])
        spf[r : r + 176, :] = got.astype(BF).astype(F32)

    def piece_state_conv():
        for q in range(4):
            acc = jnp.zeros((128, 256), F32)
            for j in range(4):
                acc = acc + cwst[j : j + 1, :] * spf[q * 128 + 13 + j : q * 128 + 13 + j + 128, :]
            v = acc * lax.logistic(acc)
            cb[q * 128 : (q + 1) * 128, :] = v[:, :128].astype(BF)
            ct[:, q * 128 : (q + 1) * 128] = v[:, 128:].T.astype(BF)

    def piece_delta():
        pre = dot(st[...], nt[:, 128:640]) + bias[:, 0:1]
        delta = jnp.maximum(pre, 0.0) + jnp.log1p(jnp.exp(-jnp.abs(pre)))
        run = -delta * rate[:, 0:1]
        lane = lax.broadcasted_iota(jnp.int32, (16, TOK), 1) % SPAN
        k = 1
        while k < SPAN:
            run = run + jnp.where(lane >= k, pltpu.roll(run, k, 1), 0.0)
            k *= 2
        cum[...] = run
        ecum[...] = jnp.exp(run)
        tot0, tot1 = run[:, 255:256], run[:, 511:512]
        tailw[:, :SPAN] = jnp.exp(tot0 - run[:, :SPAN]) * delta[:, :SPAN]
        tailw[:, SPAN:] = jnp.exp(tot1 - run[:, SPAN:]) * delta[:, SPAN:]
        d01[0] = jnp.broadcast_to(jnp.exp(tot0), (16, 128))
        d01[1] = jnp.broadcast_to(jnp.exp(tot1), (16, 128))
        whole = jnp.broadcast_to(jnp.exp(tot0) * jnp.exp(tot1), (16, 128))
        for h in range(HEADS):
            dec[8, h] = whole[h : h + 1, :]
            dec[z, h] = whole[h : h + 1, :]
        term = jnp.log(delta) - run
        filled = jnp.concatenate([term, jnp.zeros((112, TOK), F32)], axis=0)
        for q in range(4):
            colt[q * 128 : (q + 1) * 128, :] = filled[:, q * 128 : (q + 1) * 128].T
        for b in range(2):
            s = slice(b * SPAN, (b + 1) * SPAN)
            scores[b] = dot(cb[s, :], ct[:, s])

    dec_copies = []

    def piece_dec_send():
        for k in range(1, NZ):
            dec_copies.append(extra(dec.at[8], dec.at[z], dev(dz=k), k))

    def piece_dec_recv():
        for q in dec_copies:
            q.wait_recv()
        prod = dec[0]
        for k in range(1, NZ):
            prod = prod * dec[k]
        rowd[4] = prod
        rowd[y] = prod
        for k in range(1, NY):
            dec_copies.append(extra(rowd.at[4], rowd.at[y], dev(dy=k), 7 + k))

    def piece_mix(h):
        keep = lax.broadcasted_iota(jnp.int32, (128, 128), 1) >= lax.broadcasted_iota(
            jnp.int32, (128, 128), 0
        )
        for b in range(2):
            for s0 in range(2):
                r = b * SPAN + s0 * 128
                col = jnp.broadcast_to(colt[r : r + 128, h : h + 1], (128, 128))
                for t0 in range(2):
                    sl = (slice(s0 * 128, s0 * 128 + 128), slice(t0 * 128, t0 * 128 + 128))
                    if t0 < s0:
                        mix[(h, b) + sl] = jnp.zeros((128, 128), BF)
                        continue
                    q = b * SPAN + t0 * 128
                    arg = col + cum[h : h + 1, q : q + 128]
                    if s0 == t0:
                        arg = jnp.where(keep, arg, -jnp.inf)
                    mix[(h, b) + sl] = (scores[(b,) + sl] * jnp.exp(arg)).astype(BF)

    def product(h, r, first, width):
        la = wa[h, r].reshape(NZ * 40, KA)
        lb = wb[h, r].reshape(NZ * 40, KB)
        cols = slice(first, first + width)
        p0s[:, :width] = dot(la, nt[0:512, cols]) + dot(lb, nt[512:1280, cols])
        p1s[:, :width] = dot(la, nt[1280:1792, cols]) + dot(lb, nt[1792:2560, cols])

    def piece_inner(r):
        product(0, r, 0, 640)
        for i in range(NZ):
            v = p0s[40 * i : 40 * i + 20, :] + p1s[40 * i + 20 : 40 * i + 40, :]
            inn[r, 20 * i : 20 * i + 20, :] = v.astype(BF).astype(F32)

    def piece_gate(r):
        product(1, r, 128, 512)
        for i in range(NZ):
            v = p0s[40 * i : 40 * i + 20, :512] + p1s[40 * i + 20 : 40 * i + 40, :512]
            gat[r, 20 * i : 20 * i + 20, :] = v.astype(BF).astype(F32)

    def piece_conv(r):
        def step(i, carry):
            q = pl.multiple_of(i * 32, 32)
            row = pl.multiple_of(r * 160 + q, 32)
            v = inn[r, pl.ds(q, 32), :]
            w = cwin[pl.ds(row, 32), :]
            acc = w[:, 3:4] * v[:, 128:]
            for j in range(3):
                acc = acc + w[:, j : j + 1] * pltpu.roll(v, 3 - j, 1)[:, 128:]
            vt[pl.ds(row, 32), :] = (acc * lax.logistic(acc)).astype(BF)
            return carry

        lax.fori_loop(0, 5, step, 0)

    def head_rows(h):
        return pl.ds(pl.multiple_of(h * 64, 64), 64)

    def piece_update():
        def weigh(h, carry):
            vw[head_rows(h), :] = (vt[head_rows(h), :].astype(F32) * tailw[pl.ds(h, 1), :]).astype(BF)
            return carry

        lax.fori_loop(0, HEADS, weigh, 0)
        for b in range(2):
            s = slice(b * SPAN, (b + 1) * SPAN)
            u[b] = dot(vw[:, s], cb[s, :])

        def total(h, carry):
            v = u[0, head_rows(h), :] * d01[1, pl.ds(h, 1), :] + u[1, head_rows(h), :]
            for j in range(NZ):
                cs[j, h] = v[8 * j : 8 * j + 8, :].astype(BF)
            return carry

        lax.fori_loop(0, HEADS, total, 0)
        cr[z] = cs[z]

    carry1, carry2, carry3 = [], [], []

    def piece_carry1():
        for k in range(1, NZ):
            carry1.append(extra(cs.at[zz(k)], cr.at[z], dev(dz=k), 10 + k))

    def piece_carry2():
        for q in carry1:
            q.wait_recv()
        run = jnp.zeros((HEADS, 8, 128), F32)
        for k in range(NZ):
            prefix[k] = run
            run = run * dec[k] + cr[k].astype(F32)
        tt[4] = run
        tt[y] = run
        for k in range(1, NY):
            carry2.append(extra(tt.at[4], tt.at[y], dev(dy=k), 17 + k))

    def piece_carry3():
        for q in carry2 + dec_copies[7:]:
            q.wait_recv()
        r = jnp.zeros((HEADS, 8, 128), F32)
        for k in range(NY - 1):
            r = jnp.where(y > k, r * rowd[k] + tt[k], r)
        for k in range(NZ):
            co[k] = (prefix[k] + r).astype(BF)
            r = r * dec[k]
        ci[z] = co[z]
        for k in range(1, NZ):
            carry3.append(extra(co.at[zz(k)], ci.at[z], dev(dz=k), 20 + k))

    def piece_carry4():
        for q in carry3:
            q.wait_recv()

        def step(h, carry):
            v = jnp.concatenate([ci[j, h].astype(F32) for j in range(NZ)], axis=0)
            sbf[0, head_rows(h), :] = v.astype(BF)
            sbf[1, head_rows(h), :] = (v * d01[0, pl.ds(h, 1), :] + u[0, head_rows(h), :]).astype(BF)
            return carry

        lax.fori_loop(0, HEADS, step, 0)

    def piece_intra(b):
        s = slice(b * SPAN, (b + 1) * SPAN)

        def step(h, carry):
            v = vt[head_rows(h), s]
            yv[head_rows(h), s] = dot(v, mix[h, b]) + skip[h] * v.astype(F32)
            return carry

        lax.fori_loop(0, HEADS, step, 0)

    def piece_inter(b):
        s = slice(b * SPAN, (b + 1) * SPAN)

        def step(h, carry):
            got = dot(sbf[b, head_rows(h), :], ct[:, s])
            yv[head_rows(h), s] = yv[head_rows(h), s] + ecum[pl.ds(h, 1), s] * got
            return carry

        lax.fori_loop(0, HEADS, step, 0)

    pair_copies, sq_copies = [], []

    def piece_gated(b):
        s = slice(b * SPAN, (b + 1) * SPAN)
        total = jnp.zeros((8, SPAN), F32)
        for r in range(NY):

            def step(i, total):
                q = pl.multiple_of(i * 32, 32)
                row = pl.multiple_of(r * 160 + q, 32)
                g = gat[r, pl.ds(q, 32), s]
                v = yv[pl.ds(row, 32), s] * (g * lax.logistic(g))
                for e in range(4):
                    w = v[8 * e : 8 * e + 8, :]
                    total = total + w * w
                s_t[pl.ds(row, 32), s] = (v * og[pl.ds(row, 32), 0:1]).astype(BF)
                return total

            total = lax.fori_loop(0, 5, step, total)
        sq[8, :, s] = total
        for q in range(CH // 128):
            for e in range(2):
                r0 = b * SPAN + e * 128
                scb[c, r0 : r0 + 128, q * 128 : q * 128 + 128] = s_t[
                    q * 128 : q * 128 + 128, r0 : r0 + 128
                ].T
        pair_copies.append(
            extra(scb.at[c, pl.ds(b * SPAN, SPAN)], scb.at[c, pl.ds(b * SPAN, SPAN)], dev(dc=1), 28 + b)
        )

    def piece_squares():
        sq[grp] = sq[8]
        for k in range(1, 8):
            sq_copies.append(extra(sq.at[8], sq.at[grp], dev(dx=k // 2, dc=k % 2), 29 + k))

    def project(dx, half):
        s = slice(half * SPAN, (half + 1) * SPAN)
        p = xx(dx)
        return dot(scb[0, s, :], wr[p, 0:CH, :]) + dot(scb[1, s, :], wr[p, CH : 2 * CH, :])

    for q in own_in:
        q.wait()
    clock = 0.5
    progress(clock)
    front = [(functools.partial(piece_norm, i), 0.5) for i in range(4)]
    front += [(piece_halo, 0.1)]
    front += [(functools.partial(piece_transpose, i), 0.5) for i in range(5)]
    front += [(functools.partial(piece_state, i), 0.3) for i in range(3)]
    front += [(piece_state_conv, 0.3), (piece_delta, 0.6), (piece_dec_send, 0.1)]
    front += [(functools.partial(piece_mix, i), 0.25) for i in range(HEADS)]
    front += [(piece_dec_recv, 0.1)]
    for piece, cost in front:
        piece()
        clock += cost
        progress(clock)
    progress(HALF_DONE[0])
    clock = HALF_DONE[0]
    complete(0)
    middle = []
    for i in range(NY):
        middle += [(functools.partial(piece_inner, i), 1.0), (functools.partial(piece_conv, i), 0.4)]
    middle += [(piece_update, 0.6), (piece_carry1, 0.1)]
    middle += [(functools.partial(piece_intra, i), 0.8) for i in range(2)]
    for piece, cost in middle:
        piece()
        clock += cost
        progress(clock)
    clock += 3.0
    progress(clock)
    piece_carry2()
    clock += 4.0
    progress(clock)
    piece_carry3()
    clock += 5.0
    progress(clock)
    piece_carry4()
    for i in range(2):
        piece_inter(i)
        clock += 0.4
        progress(clock)
    progress(1e9)
    complete(1)
    for i in range(NY):
        piece_gate(i)
    for i in range(2):
        piece_gated(i)
    piece_squares()
    own_out.wait()
    for k in (("X1", 1), ("X1", -1), ("X2f", 1), ("X2f", -1)):
        take(k)
    for q in pair_copies:
        q.wait_recv()
    far = []
    for half, d in ((0, 1), (1, -1)):
        rs_out[half] = project(2, half).astype(BF)
        far.append(extra(rs_out.at[half], rs_in1.at[half], dev(dx=d), 40 + half))
    near = []
    for i, d in enumerate((1, -1)):
        direct = 1 if d == 1 else 0
        rs2_out[i, direct] = project(d, direct).astype(BF)
        near.append(extra(rs2_out.at[i, direct], rs2_in.at[i, direct], dev(dx=d), 42 + 2 * i))
    for i, d in enumerate((1, -1)):
        relayed = 0 if d == 1 else 1
        v = project(d, relayed)
        far[relayed].wait_recv()
        rs2_out[i, relayed] = (v + rs_in1[relayed].astype(F32)).astype(BF)
        near.append(extra(rs2_out.at[i, relayed], rs2_in.at[i, relayed], dev(dx=d), 43 + 2 * i))
    for half in range(2):
        own_p[half] = project(0, half)
    for q in sq_copies:
        q.wait_recv()
    total = sq[0]
    for k in range(1, 8):
        total = total + sq[k]
    total = jnp.sum(total, axis=0, keepdims=True)
    scale = lax.rsqrt(total / (8 * CH) + EPS)
    scale = jnp.broadcast_to(scale, (128, TOK))
    for q in near:
        q.wait_recv()
    for half in range(2):
        v = own_p[half] + rs2_in[0, half].astype(F32) + rs2_in[1, half].astype(F32)
        for e in range(2):
            r0 = half * SPAN + e * 128
            column = scale[:, r0 : r0 + 128].T[:, 0:1]
            out[r0 : r0 + 128, :] = (v[e * 128 : e * 128 + 128, :] * column).astype(BF)
    for k in MSGS:
        message(k).wait_send()
    for q in extra_sends:
        q.wait_send()


def run(*args):
    vm = pl.BlockSpec(memory_space=pltpu.VMEM)
    specs = [vm] * 13
    specs[8] = pl.BlockSpec(memory_space=pltpu.SMEM)
    specs[12] = pl.BlockSpec(memory_space=pl.ANY)
    V = pltpu.VMEM
    scratch = [
        V((2, NY, NZ, 40, KA), BF),
        V((2, NY, NZ, 40, KB), BF),
        V((640, D), BF),
        V((D, 640), BF),
        V((528, 256), F32),
        V((TOK, 128), BF),
        V((128, TOK), BF),
        V((9, HEADS, 1, 128), F32),
        V((16, TOK), F32),
        V((16, TOK), F32),
        V((16, TOK), F32),
        V((2, 16, 128), F32),
        V((2, SPAN, SPAN), F32),
        V((HEADS, 2, SPAN, SPAN), BF),
        V((TOK, 128), F32),
        V((320, 640), F32),
        V((320, 640), F32),
        V((NY, 160, 640), F32),
        V((NY, 160, TOK), F32),
        V((CH, TOK), BF),
        V((CH, TOK), BF),
        V((2, CH, 128), F32),
        V((CH, TOK), F32),
        V((NZ, HEADS, 8, 128), BF),
        V((NZ, HEADS, 8, 128), BF),
        V((NZ, HEADS, 8, 128), BF),
        V((NZ, HEADS, 8, 128), BF),
        V((5, HEADS, 8, 128), F32),
        V((5, HEADS, 1, 128), F32),
        V((NZ, HEADS, 8, 128), F32),
        V((2, CH, 128), BF),
        V((CH, TOK), BF),
        V((2, TOK, CH), BF),
        V((NX, 1280, FEAT), BF),
        V((2, 640, FEAT), BF),
        V((9, 8, TOK), F32),
        V((2, SPAN, FEAT), BF),
        V((2, SPAN, FEAT), BF),
        V((2, 2, SPAN, FEAT), BF),
        V((2, 2, SPAN, FEAT), BF),
        V((2, SPAN, FEAT), F32),
        V((16, D), BF),
        pltpu.SemaphoreType.DMA((N_MSG,)),
        pltpu.SemaphoreType.DMA((N_MSG,)),
        pltpu.SemaphoreType.DMA((48,)),
        pltpu.SemaphoreType.DMA((48,)),
        pltpu.SemaphoreType.DMA((5,)),
    ]
    return pl.pallas_call(
        kernel,
        out_shape=jax.ShapeDtypeStruct((TOK, FEAT), BF),
        in_specs=specs,
        out_specs=vm,
        scratch_shapes=scratch,
        compiler_params=pltpu.CompilerParams(
            collective_id=0, has_side_effects=True, vmem_limit_bytes=64 * 2**20 - 65536
        ),
        name="layer",
    )(*args)


def body(
    tokens, norm_gain, inner_weight, state_weight, step_weight, step_bias, decay_rate,
    skip_scale, conv_inner, conv_state, out_gain, out_weight,
):
    folded = inner_weight.transpose(1, 2, 0).reshape(2, 20, 2, D // 2)
    folded = folded.transpose(0, 2, 1, 3).reshape(2, 40, D // 2)
    steps = jnp.pad(step_weight.T, ((0, 6), (0, 0)))

    def columns(v):
        return jnp.broadcast_to(jnp.pad(v, (0, 6))[:, None], (16, 128))

    return run(
        tokens,
        norm_gain[None, :],
        folded[:, :, :KA],
        folded[:, :, KA:],
        state_weight.reshape(D, 256),
        steps,
        columns(step_bias),
        columns(decay_rate),
        skip_scale,
        conv_inner.T.astype(F32),
        conv_state.reshape(4, 256).astype(F32),
        out_gain[:, None],
        out_weight,
    )


def solution(mesh):
    return jax.shard_map(
        body,
        mesh=mesh,
        in_specs=(
            P("seq", None), P(), P(None, None, ("grp", "seq")), P(), P(None, "grp"), P("grp"),
            P("grp"), P("grp"), P(None, "grp"), P(), P("grp"), P(None, "grp"),
        ),
        out_specs=P("seq", "grp"),
        check_vma=False,
    )
```

time: 291 us -> 125 us (0.43); the launches traced: 287 us -> 125 us
  waiting for transfers between devices: 135 us -> 0 us
  Pallas kernels: 0 us -> 104 us
  blocking collectives: 35.8 us -> 0 us
  local copies, waits for them, and re-layouts: 52.7 us -> 20.1 us
  matrix products: 18.9 us -> 0 us
  starting transfers between devices: 18.7 us -> 0 us
  between operations: 13.5 us -> 0.04 us
  other arithmetic: 12.3 us -> 0.68 us
    pallas_call x0 -> x1, Pallas kernels: none -> 104 us  [run(): pl.pallas_call(kernel, out_shape=jax.ShapeDtypeStruct((TOK, FEAT), BF), i...]
    all_gather x3 -> x0, waiting for transfers between devices: 98.6 us -> none  [the longest x1 72.6 us: body(): piece = lax.all_gather(inner_weight, SEQ, axis=2, tiled=True)]
    dynamic_update_slice x4 -> x0, local copies, waits for them, and re-layouts: 29.6 us -> none  [body(): lax.scan(partial(span_step, decay_rate, skip_scale), initial, (xs_blocks,...]
    reduce_scatter x1 -> x0, waiting for transfers between devices: 28.3 us -> none  [body(): lax.psum_scatter(partial_sums, 'grp', scatter_dimension=1, tiled=True)]
    all_gather x2 -> x0, blocking collectives: 22.3 us -> none  [carried_in(): pieces = jax.tree.map(lambda part: lax.all_gather(part, axis), total)]
    dot_general x13 -> x0, matrix products: 18.9 us -> none  [the longest x1 5.6 us: body(): jnp.dot(scaled, regrouped, preferred_element_type=jnp.float32)]
    all_to_all x2 -> x0, starting transfers between devices: 14.5 us -> none  [the longest x1 7.94 us: body(): lax.all_to_all(out_weight, 'grp', split_axis=0, concat_axis=1, tiled=True)]
    psum x1 -> x0, blocking collectives: 13.5 us -> none  [body(): squares = lax.psum(jnp.sum(gated * gated, axis=1), 'grp')]
  transfers between devices with their start and end apart: 8 -> 0, of which waited for: 7 -> 0; matrix products, arithmetic and copies ran while one was open for 10% -> 0% of each run, Pallas kernels for 0% -> 0%
where the time goes in v1:
time: 125 us
  Pallas kernels  104 us (83%)
  local copies, waits for them, and re-layouts  20.1 us (16%)
    pallas_call x1, Pallas kernels, run(): pl.pallas_call(kernel, out_shape=jax.ShapeDtypeStruct((TOK, FEAT), BF), i...  104 us
    unnamed x7, local copies, waits for them, and re-layouts  8.11 us

profile of v1, /device:TPU:1, one launch (start us, length us, event | category | flops | bytes accessed | tf_op | source)
XLA Modules:
  0.0 125.2 jit_solution(11161387907969915233)
XLA Ops:
  0.0 0.0 copy-start
  0.0 0.8 pad.12
  0.8 0.8 pad.13
  1.6 0.7 convert_bitcast_fusion
  2.3 0.6 copy.34
  2.9 0.7 broadcast_in_dim.20.rate
  3.6 0.7 broadcast_in_dim.9.bias
  4.2 1.3 %broadcast_in_dim.8.gain = f32[1,2560]{1,0:T(1,128)} reshape(f32[2560]{0:T(1024)} %param.13) | data formatting | bytes 20480 | tf_op jit(solution)/shard_map/broadcast_in_dim | solution.py:679
  5.5 1.5 %pad.11.st = bf16[16,2560]{1,0:T(8,128)(2,1)} pad(bf16[10,2560]{1,0:T(8,128)(2,1)} %bitcast.25, bf16[]{:T(256)} %constant.3.clone.1), padding=0_6x0_0 | pad | bytes 133122 | tf_op jit(solution)/shard_map/jit(_pad)/pad | solution.py:672
  7.1 1.1 copy.33
  8.1 0.1 slice.8
  8.2 0.1 slice.9
  8.3 0.7 copy.25.own_b
  9.0 0.6 copy.24.own_a
  9.6 1.6 %copy.20 = f32[4,640]{0,1:T(8,128)} copy(bf16[4,640]{1,0:T(4,128)(2,1)} %param.20) | data formatting | bytes 15360 | tf_op jit(solution)/shard_map/convert_element_type | solution.py:687
  11.2 1.6 %broadcast_in_dim.22.og = f32[640,1]{1,0:T(8,128)} reshape(f32[640]{0:T(1024)} %param.22) | data formatting | bytes 5120 | tf_op jit(solution)/shard_map/broadcast_in_dim | solution.py:689
  12.8 2.6 %copy.32 = bf16[320,8,2,128]{3,1,2,0:T(8,128)(2,1)} copy(bf16[320,8,2,128]{3,2,1,0:T(2,128)(2,1)} %bitcast.21) | data formatting | bytes 2621440
  15.3 0.0 copy-done
  15.3 3.6 %copy.22.ow = bf16[5120,320]{1,0:T(8,128)(2,1)} copy(bf16[5120,320]{0,1:T(8,128)(2,1)S(1)} %copy-done) | data formatting | bytes 6553600 | tf_op args[11]
  19.0 104.3 %layer.1 = bf16[512,320]{1,0:T(8,128)(2,1)} custom-call(bf16[512,2560]{1,0:T(8,128)(2,1)} %tok.1, f32[1,2560]{1,0:T(1,128)} %broadcast_in_dim.8.gain, bf16[2,40,512]{2,1,0:T(8,128)(2,1)} %copy.24.own_a, bf16[2,40,768]{2,1,0:T(8,128)(2,1)} %copy.25.own_b, bf16[2560,256]{1,0:T(8,128)(2,1)} %bitcast.19, bf16[16,2560]{1,0:T(8,128)(2,1)} %pad.11.st, ...), custom_call_target="tpu_custom_call" | custom-call | tf_op jit(solution)/shard_map/layer/pallas_call | solution.py:653
  123.3 1.9 %copy.23 = bf16[512,320]{0,1:T(8,128)(2,1)} copy(bf16[512,320]{1,0:T(8,128)(2,1)} %layer.1) | data formatting | bytes 655360 | tf_op jit(solution)/shard_map/layer/pallas_call | solution.py:653
Async XLA Ops:
  0.0 15.3 %copy-start = (bf16[5120,320]{0,1:T(8,128)(2,1)S(1)}, bf16[5120,320]{0,1:T(8,128)(2,1)}, u32[]{:S(2)}) copy-start(bf16[5120,320]{0,1:T(8,128)(2,1)} %param.23) | copy-start | bytes 9830404

commit v2 on v1

--- a/solution.py
+++ b/solution.py
@@ -110,11 +110,11 @@
 
 
 def kernel(
-    tok, gain, own_a, own_b, sw, st, bias, rate, skip, cwin, cwst, og, ow,
+    tok_in, gain, own_in, sw_in, st, bias, rate, skip, cw_in, cwst, og_in, ow,
     out,
-    wa, wb, nrm, nt, spf, cb, ct, dec, cum, ecum, tailw, d01, scores, mix, colt,
+    tok, own_a, own_b, own_f, sw, swd, cwin, og, wa, wb, nrm, nt, spf, cb, ct, dec, cum, ecum, tailw, d01, scores, mix, term, colt,
     p0s, p1s, inn, gat, vt, vw, u, yv, cs, cr, co, ci, tt, rowd, prefix,
-    sbf, s_t, scb, wr, relay, sq, rs_out, rs_in1, rs2_out, rs2_in, own_p,
+    sbf, scb, wr, relay, sq, rs_out, rs_in1, rs2_out, rs2_in, own_p,
     halo, send, recv, xsend, xrecv, lsem,
 ):
     seq = lax.axis_index("seq")
@@ -145,18 +145,34 @@
     for p in peers:
         pl.semaphore_signal(barrier, inc=1, device_id=p, device_id_type=MESH)
 
-    own_out = pltpu.make_async_copy(
-        ow.at[pl.ds(pl.multiple_of(x * 1280, 1280), 1280)], wr.at[x], lsem.at[0]
-    )
+    def feature_columns(d, first, count):
+        return ow.at[:, pl.ds(pl.multiple_of(xx(d) * 1280 + first, 128), count)]
+
+    tok_copies = []
+    for q in range(4):
+        part = pl.ds(q * 128, 128)
+        tok_copies.append(pltpu.make_async_copy(tok_in.at[part], tok.at[part], lsem.at[q]))
+        tok_copies[q].start()
+    sw_copy = pltpu.make_async_copy(sw_in, sw, lsem.at[4])
+    sw_copy.start()
+    own_out = pltpu.make_async_copy(feature_columns(0, 0, 1280), wr.at[x], lsem.at[5])
     own_out.start()
-    own_in = []
+    for r in range(20):
+        v = own_in[r].astype(F32)
+        for h in (0, 1):
+            for part in (0, 1):
+                own_f[h, 20 * part + r : 20 * part + r + 1, :] = v[
+                    h : h + 1, part * (D // 2) : (part + 1) * (D // 2)
+                ]
     for h in (0, 1):
-        own_in.append(pltpu.make_async_copy(own_a.at[h], wa.at[h, y, z], lsem.at[1 + h]))
-        own_in.append(pltpu.make_async_copy(own_b.at[h], wb.at[h, y, z], lsem.at[3 + h]))
-    for q in own_in:
-        q.start()
+        v = own_f[h].astype(BF)
+        own_a[h] = v[:, :KA]
+        own_b[h] = v[:, KA:]
+        wa[h, y, z] = v[:, :KA]
+        wb[h, y, z] = v[:, KA:]
     nrm[0:128, :] = jnp.zeros((128, D), BF)
-    pl.semaphore_wait(barrier, len(peers))
+    with jax.named_scope("barrier"):
+        pl.semaphore_wait(barrier, len(peers))
 
     def remote(src, dst, s, r, to):
         return pltpu.make_async_remote_copy(
@@ -169,16 +185,15 @@
         if kind[0] == "X":
             d = k[1]
             if kind == "X1":
-                src = ow.at[pl.ds(pl.multiple_of(xx(d) * 1280, 1280), 1280)]
-                dst = wr.at[x]
+                src, dst = feature_columns(d, 0, 1280), wr.at[x]
             elif kind == "X2":
                 off = 0 if d == 1 else 640
-                src = ow.at[pl.ds(pl.multiple_of(xx(2) * 1280, 1280) + off, 640)]
+                src = feature_columns(2, off, 640)
                 dst = relay.at[0 if d == 1 else 1]
             else:
                 off = 0 if d == 1 else 640
                 src = relay.at[0 if d == 1 else 1]
-                dst = wr.at[xx(-d), pl.ds(off, 640)]
+                dst = wr.at[xx(-d), :, pl.ds(off, 640)]
             return remote(src, dst, send.at[i], recv.at[i], dev(dx=d))
         h, d = k[1], k[2]
         if kind == "Ay":
@@ -238,14 +253,16 @@
         extra_sends.append(q)
         return q
 
-    halo_copy = extra(tok.at[pl.ds(TOK - 16, 16)], halo, nxt, 0)
+    halo_copy = extra(tok_in.at[pl.ds(TOK - 16, 16)], halo, nxt, 0)
 
     def norm_rows(v):
         wide = v.astype(F32)
         ms = jnp.mean(wide * wide, axis=1, keepdims=True)
-        return wide * lax.rsqrt(ms + EPS) * gain[...]
+        return wide * lax.rsqrt(ms + EPS) * gain[...].reshape(1, D)
 
     def piece_norm(part):
+        tok_copies[part].wait()
+
         def step(i, carry):
             r = pl.multiple_of(part * 128 + i * 16, 16)
             nrm[pl.ds(128 + r, 16), :] = norm_rows(tok[pl.ds(r, 16), :]).astype(BF)
@@ -268,25 +285,47 @@
 
         lax.fori_loop(0, D // 128, step, 0)
 
+    def piece_state_weight():
+        sw_copy.wait()
+
+        def step(i, carry):
+            r = pl.multiple_of(i * 128, 128)
+            v = sw[pl.ds(r, 128), :, :].astype(F32)
+            swd[pl.ds(r, 128), 0:128] = v[:, 0, :].astype(BF)
+            swd[pl.ds(r, 128), 128:256] = v[:, 1, :].astype(BF)
+            return carry
+
+        lax.fori_loop(0, D // 128, step, 0)
+
     def piece_state(part):
         r = part * 176
-        got = dot(nrm[112 + r : 112 + r + 176, :], sw[...])
+        got = dot(nrm[112 + r : 112 + r + 176, :], swd[...])
         spf[r : r + 176, :] = got.astype(BF).astype(F32)
 
     def piece_state_conv():
         for q in range(4):
-            acc = jnp.zeros((128, 256), F32)
-            for j in range(4):
-                acc = acc + cwst[j : j + 1, :] * spf[q * 128 + 13 + j : q * 128 + 13 + j + 128, :]
-            v = acc * lax.logistic(acc)
-            cb[q * 128 : (q + 1) * 128, :] = v[:, :128].astype(BF)
-            ct[:, q * 128 : (q + 1) * 128] = v[:, 128:].T.astype(BF)
+            for k in (0, 1):
+                acc = jnp.zeros((128, 128), F32)
+                for j in range(4):
+                    first = q * 128 + 13 + j
+                    w = cwst[j].astype(F32)[k : k + 1, :]
+                    acc = acc + w * spf[first : first + 128, k * 128 : (k + 1) * 128]
+                v = acc * lax.logistic(acc)
+                if k == 0:
+                    cb[q * 128 : (q + 1) * 128, :] = v.astype(BF)
+                else:
+                    ct[:, q * 128 : (q + 1) * 128] = v.T.astype(BF)
 
     def piece_delta():
-        pre = dot(st[...], nt[:, 128:640]) + bias[:, 0:1]
+        row = lax.broadcasted_iota(jnp.int32, (HEADS, TOK), 0)
+        bias_col = rate_col = jnp.zeros((HEADS, TOK), F32)
+        for h in range(HEADS):
+            bias_col = jnp.where(row == h, bias[h], bias_col)
+            rate_col = jnp.where(row == h, rate[h], rate_col)
+        pre = dot(st[...], nt[:, 128:640]) + bias_col
         delta = jnp.maximum(pre, 0.0) + jnp.log1p(jnp.exp(-jnp.abs(pre)))
-        run = -delta * rate[:, 0:1]
-        lane = lax.broadcasted_iota(jnp.int32, (16, TOK), 1) % SPAN
+        run = -delta * rate_col
+        lane = lax.broadcasted_iota(jnp.int32, (HEADS, TOK), 1) % SPAN
         k = 1
         while k < SPAN:
             run = run + jnp.where(lane >= k, pltpu.roll(run, k, 1), 0.0)
@@ -296,16 +335,16 @@
         tot0, tot1 = run[:, 255:256], run[:, 511:512]
         tailw[:, :SPAN] = jnp.exp(tot0 - run[:, :SPAN]) * delta[:, :SPAN]
         tailw[:, SPAN:] = jnp.exp(tot1 - run[:, SPAN:]) * delta[:, SPAN:]
-        d01[0] = jnp.broadcast_to(jnp.exp(tot0), (16, 128))
-        d01[1] = jnp.broadcast_to(jnp.exp(tot1), (16, 128))
-        whole = jnp.broadcast_to(jnp.exp(tot0) * jnp.exp(tot1), (16, 128))
+        d01[0] = jnp.broadcast_to(jnp.exp(tot0), (HEADS, 128))
+        d01[1] = jnp.broadcast_to(jnp.exp(tot1), (HEADS, 128))
+        whole = jnp.broadcast_to(jnp.exp(tot0) * jnp.exp(tot1), (HEADS, 128))
         for h in range(HEADS):
             dec[8, h] = whole[h : h + 1, :]
             dec[z, h] = whole[h : h + 1, :]
-        term = jnp.log(delta) - run
-        filled = jnp.concatenate([term, jnp.zeros((112, TOK), F32)], axis=0)
+        term[...] = jnp.zeros((128, TOK), F32)
+        term[0:HEADS, :] = jnp.log(delta) - run
         for q in range(4):
-            colt[q * 128 : (q + 1) * 128, :] = filled[:, q * 128 : (q + 1) * 128].T
+            colt[q * 128 : (q + 1) * 128, :] = term[:, q * 128 : (q + 1) * 128].T
         for b in range(2):
             s = slice(b * SPAN, (b + 1) * SPAN)
             scores[b] = dot(cb[s, :], ct[:, s])
@@ -479,20 +518,13 @@
                 for e in range(4):
                     w = v[8 * e : 8 * e + 8, :]
                     total = total + w * w
-                s_t[pl.ds(row, 32), s] = (v * og[pl.ds(row, 32), 0:1]).astype(BF)
+                scb[c, pl.ds(row, 32), s] = (v * og[pl.ds(row, 32), 0:1]).astype(BF)
                 return total
 
             total = lax.fori_loop(0, 5, step, total)
         sq[8, :, s] = total
-        for q in range(CH // 128):
-            for e in range(2):
-                r0 = b * SPAN + e * 128
-                scb[c, r0 : r0 + 128, q * 128 : q * 128 + 128] = s_t[
-                    q * 128 : q * 128 + 128, r0 : r0 + 128
-                ].T
-        pair_copies.append(
-            extra(scb.at[c, pl.ds(b * SPAN, SPAN)], scb.at[c, pl.ds(b * SPAN, SPAN)], dev(dc=1), 28 + b)
-        )
+        own = scb.at[c, :, pl.ds(b * SPAN, SPAN)]
+        pair_copies.append(extra(own, own, dev(dc=1), 28 + b))
 
     def piece_squares():
         sq[grp] = sq[8]
@@ -502,77 +534,97 @@
     def project(dx, half):
         s = slice(half * SPAN, (half + 1) * SPAN)
         p = xx(dx)
-        return dot(scb[0, s, :], wr[p, 0:CH, :]) + dot(scb[1, s, :], wr[p, CH : 2 * CH, :])
-
-    for q in own_in:
-        q.wait()
+        return dot(wr[p, :, 0:CH], scb[0, :, s]) + dot(wr[p, :, CH : 2 * CH], scb[1, :, s])
+
+    def piece_gains():
+        term[...] = jnp.zeros((128, TOK), F32)
+        for q in range(CH // 128):
+            cols = slice(q * 128, q * 128 + 128)
+            term[0:4, 0:128] = cw_in[:, cols].astype(F32)
+            cwin[cols, :] = term[:, 0:128].T
+            og[cols, :] = jnp.broadcast_to(og_in[cols].reshape(1, 128), (128, 128)).T
+
+    def piece_name(piece):
+        inside = getattr(piece, "func", piece)
+        return inside.__name__ + "".join(f"#i={a}" for a in getattr(piece, "args", ()))
+
+    def call(piece, *args):
+        with jax.named_scope(piece.__name__ + "".join(f"#i={a}" for a in args)):
+            return piece(*args)
+
     clock = 0.5
     progress(clock)
     front = [(functools.partial(piece_norm, i), 0.5) for i in range(4)]
-    front += [(piece_halo, 0.1)]
+    front += [(piece_halo, 0.1), (piece_gains, 0.4)]
     front += [(functools.partial(piece_transpose, i), 0.5) for i in range(5)]
+    front += [(piece_state_weight, 1.0)]
     front += [(functools.partial(piece_state, i), 0.3) for i in range(3)]
     front += [(piece_state_conv, 0.3), (piece_delta, 0.6), (piece_dec_send, 0.1)]
     front += [(functools.partial(piece_mix, i), 0.25) for i in range(HEADS)]
     front += [(piece_dec_recv, 0.1)]
     for piece, cost in front:
-        piece()
+        with jax.named_scope(piece_name(piece)):
+            piece()
         clock += cost
         progress(clock)
     progress(HALF_DONE[0])
     clock = HALF_DONE[0]
-    complete(0)
+    call(complete, 0)
     middle = []
     for i in range(NY):
         middle += [(functools.partial(piece_inner, i), 1.0), (functools.partial(piece_conv, i), 0.4)]
     middle += [(piece_update, 0.6), (piece_carry1, 0.1)]
     middle += [(functools.partial(piece_intra, i), 0.8) for i in range(2)]
     for piece, cost in middle:
-        piece()
+        with jax.named_scope(piece_name(piece)):
+            piece()
         clock += cost
         progress(clock)
     clock += 3.0
     progress(clock)
-    piece_carry2()
+    call(piece_carry2)
     clock += 4.0
     progress(clock)
-    piece_carry3()
+    call(piece_carry3)
     clock += 5.0
     progress(clock)
-    piece_carry4()
+    call(piece_carry4)
     for i in range(2):
-        piece_inter(i)
+        call(piece_inter, i)
         clock += 0.4
         progress(clock)
     progress(1e9)
-    complete(1)
+    call(complete, 1)
     for i in range(NY):
-        piece_gate(i)
+        call(piece_gate, i)
     for i in range(2):
-        piece_gated(i)
-    piece_squares()
-    own_out.wait()
-    for k in (("X1", 1), ("X1", -1), ("X2f", 1), ("X2f", -1)):
-        take(k)
-    for q in pair_copies:
-        q.wait_recv()
+        call(piece_gated, i)
+    call(piece_squares)
+    with jax.named_scope("wait_weights"):
+        own_out.wait()
+        for k in (("X1", 1), ("X1", -1), ("X2f", 1), ("X2f", -1)):
+            take(k)
+    with jax.named_scope("wait_pair"):
+        for q in pair_copies:
+            q.wait_recv()
     far = []
     for half, d in ((0, 1), (1, -1)):
-        rs_out[half] = project(2, half).astype(BF)
+        rs_out[half] = call(project, 2, half).astype(BF)
         far.append(extra(rs_out.at[half], rs_in1.at[half], dev(dx=d), 40 + half))
     near = []
     for i, d in enumerate((1, -1)):
         direct = 1 if d == 1 else 0
-        rs2_out[i, direct] = project(d, direct).astype(BF)
+        rs2_out[i, direct] = call(project, d, direct).astype(BF)
         near.append(extra(rs2_out.at[i, direct], rs2_in.at[i, direct], dev(dx=d), 42 + 2 * i))
     for i, d in enumerate((1, -1)):
         relayed = 0 if d == 1 else 1
-        v = project(d, relayed)
-        far[relayed].wait_recv()
+        v = call(project, d, relayed)
+        with jax.named_scope("wait_far"):
+            far[relayed].wait_recv()
         rs2_out[i, relayed] = (v + rs_in1[relayed].astype(F32)).astype(BF)
         near.append(extra(rs2_out.at[i, relayed], rs2_in.at[i, relayed], dev(dx=d), 43 + 2 * i))
     for half in range(2):
-        own_p[half] = project(0, half)
+        own_p[half] = call(project, 0, half)
     for q in sq_copies:
         q.wait_recv()
     total = sq[0]
@@ -580,28 +632,37 @@
         total = total + sq[k]
     total = jnp.sum(total, axis=0, keepdims=True)
     scale = lax.rsqrt(total / (8 * CH) + EPS)
-    scale = jnp.broadcast_to(scale, (128, TOK))
-    for q in near:
-        q.wait_recv()
+    with jax.named_scope("wait_near"):
+        for q in near:
+            q.wait_recv()
     for half in range(2):
         v = own_p[half] + rs2_in[0, half].astype(F32) + rs2_in[1, half].astype(F32)
-        for e in range(2):
-            r0 = half * SPAN + e * 128
-            column = scale[:, r0 : r0 + 128].T[:, 0:1]
-            out[r0 : r0 + 128, :] = (v[e * 128 : e * 128 + 128, :] * column).astype(BF)
-    for k in MSGS:
-        message(k).wait_send()
+        s = slice(half * SPAN, (half + 1) * SPAN)
+        out[:, s] = (v * scale[:, s]).astype(BF)
+    with jax.named_scope("wait_sends"):
+        for k in MSGS:
+            message(k).wait_send()
     for q in extra_sends:
         q.wait_send()
 
 
 def run(*args):
     vm = pl.BlockSpec(memory_space=pltpu.VMEM)
-    specs = [vm] * 13
-    specs[8] = pl.BlockSpec(memory_space=pltpu.SMEM)
-    specs[12] = pl.BlockSpec(memory_space=pl.ANY)
+    specs = [vm] * 12
+    for i in (5, 6, 7):
+        specs[i] = pl.BlockSpec(memory_space=pltpu.SMEM)
+    for i in (0, 3, 11):
+        specs[i] = pl.BlockSpec(memory_space=pl.ANY)
     V = pltpu.VMEM
     scratch = [
+        V((TOK, D), BF),
+        V((2, 40, KA), BF),
+        V((2, 40, KB), BF),
+        V((2, 40, D // 2), F32),
+        V((D, 2, 128), BF),
+        V((D, 256), BF),
+        V((CH, 128), F32),
+        V((CH, 128), F32),
         V((2, NY, NZ, 40, KA), BF),
         V((2, NY, NZ, 40, KB), BF),
         V((640, D), BF),
@@ -610,12 +671,13 @@
         V((TOK, 128), BF),
         V((128, TOK), BF),
         V((9, HEADS, 1, 128), F32),
-        V((16, TOK), F32),
-        V((16, TOK), F32),
-        V((16, TOK), F32),
-        V((2, 16, 128), F32),
+        V((HEADS, TOK), F32),
+        V((HEADS, TOK), F32),
+        V((HEADS, TOK), F32),
+        V((2, HEADS, 128), F32),
         V((2, SPAN, SPAN), F32),
         V((HEADS, 2, SPAN, SPAN), BF),
+        V((128, TOK), F32),
         V((TOK, 128), F32),
         V((320, 640), F32),
         V((320, 640), F32),
@@ -633,26 +695,25 @@
         V((5, HEADS, 1, 128), F32),
         V((NZ, HEADS, 8, 128), F32),
         V((2, CH, 128), BF),
-        V((CH, TOK), BF),
-        V((2, TOK, CH), BF),
-        V((NX, 1280, FEAT), BF),
-        V((2, 640, FEAT), BF),
+        V((2, CH, TOK), BF),
+        V((NX, FEAT, 1280), BF),
+        V((2, FEAT, 640), BF),
         V((9, 8, TOK), F32),
-        V((2, SPAN, FEAT), BF),
-        V((2, SPAN, FEAT), BF),
-        V((2, 2, SPAN, FEAT), BF),
-        V((2, 2, SPAN, FEAT), BF),
-        V((2, SPAN, FEAT), F32),
+        V((2, FEAT, SPAN), BF),
+        V((2, FEAT, SPAN), BF),
+        V((2, 2, FEAT, SPAN), BF),
+        V((2, 2, FEAT, SPAN), BF),
+        V((2, FEAT, SPAN), F32),
         V((16, D), BF),
         pltpu.SemaphoreType.DMA((N_MSG,)),
         pltpu.SemaphoreType.DMA((N_MSG,)),
         pltpu.SemaphoreType.DMA((48,)),
         pltpu.SemaphoreType.DMA((48,)),
-        pltpu.SemaphoreType.DMA((5,)),
+        pltpu.SemaphoreType.DMA((6,)),
     ]
     return pl.pallas_call(
         kernel,
-        out_shape=jax.ShapeDtypeStruct((TOK, FEAT), BF),
+        out_shape=jax.ShapeDtypeStruct((FEAT, TOK), BF),
         in_specs=specs,
         out_specs=vm,
         scratch_shapes=scratch,
@@ -667,28 +728,10 @@
     tokens, norm_gain, inner_weight, state_weight, step_weight, step_bias, decay_rate,
     skip_scale, conv_inner, conv_state, out_gain, out_weight,
 ):
-    folded = inner_weight.transpose(1, 2, 0).reshape(2, 20, 2, D // 2)
-    folded = folded.transpose(0, 2, 1, 3).reshape(2, 40, D // 2)
-    steps = jnp.pad(step_weight.T, ((0, 6), (0, 0)))
-
-    def columns(v):
-        return jnp.broadcast_to(jnp.pad(v, (0, 6))[:, None], (16, 128))
-
     return run(
-        tokens,
-        norm_gain[None, :],
-        folded[:, :, :KA],
-        folded[:, :, KA:],
-        state_weight.reshape(D, 256),
-        steps,
-        columns(step_bias),
-        columns(decay_rate),
-        skip_scale,
-        conv_inner.T.astype(F32),
-        conv_state.reshape(4, 256).astype(F32),
-        out_gain[:, None],
-        out_weight,
-    )
+        tokens, norm_gain, inner_weight.transpose(2, 1, 0), state_weight, step_weight.T,
+        step_bias, decay_rate, skip_scale, conv_inner, conv_state, out_gain, out_weight.T,
+    ).T
 
 
 def solution(mesh):

time: 125 us -> 105 us (0.84)
  local copies, waits for them, and re-layouts: 20.1 us -> 1.72 us
    unnamed x7 -> x1, local copies, waits for them, and re-layouts: 8.11 us -> 1.72 us
    broadcast_in_dim x4 -> x0, local copies, waits for them, and re-layouts: 4.2 us -> none  [the longest x1 1.58 us: body(): out_gain[:, None]]
    pad x3 -> x0, local copies, waits for them, and re-layouts: 3.16 us -> none  [the longest x2 1.63 us: columns(): return jnp.broadcast_to(jnp.pad(v, (0, 6))[:, None], (16, 128))]
    pallas_call x1 -> x0, local copies, waits for them, and re-layouts: 1.88 us -> none  [run(): pl.pallas_call(kernel, out_shape=jax.ShapeDtypeStruct((TOK, FEAT), BF), i...]
    convert_element_type x1 -> x0, local copies, waits for them, and re-layouts: 1.57 us -> none  [body(): conv_inner.T.astype(F32)]
    pallas_call x1, Pallas kernels: 104 us -> 103 us  [run(): pl.pallas_call(kernel, out_shape=jax.ShapeDtypeStruct((FEAT, TOK), BF), i...]
where the time goes in v2:
time: 105 us
  Pallas kernels  103 us (98%)
  local copies, waits for them, and re-layouts  1.72 us (2%)
    pallas_call x1, Pallas kernels, run(): pl.pallas_call(kernel, out_shape=jax.ShapeDtypeStruct((FEAT, TOK), BF), i...  103 us

profile of v2, /device:TPU:1, one launch (start us, length us, event | category | flops | bytes accessed | tf_op | source)
XLA Modules:
  0.0 104.6 jit_solution(10737997000927505963)
XLA Ops:
  0.0 102.8 %layer.1 = bf16[320,512]{1,0:T(8,128)(2,1)} custom-call(bf16[512,2560]{1,0:T(8,128)(2,1)} %tok_in.1, f32[2560]{0:T(1024)} %gain.1, bf16[20,2,2560]{2,1,0:T(2,128)(2,1)} %bitcast.6, bf16[2560,2,128]{2,1,0:T(2,128)(2,1)} %sw_in.1, bf16[10,2560]{1,0:T(8,128)(2,1)} %bitcast.7, f32[10]{0:T(128)} %bias.1, f32[10]{0:T(128)} %rate.1, f32[10]{0:T(128)} %skip.1, ...), custom_call_target="tpu_custom_call" | custom-call | tf_op jit(solution)/shard_map/layer/pallas_call | solution.py:714
  102.8 1.7 %copy.14 = bf16[512,320]{0,1:T(8,128)(2,1)} copy(bf16[512,320]{0,1:T(8,128)(2,1)} %bitcast.5) | data formatting | bytes 655360

commit v3 on v2

--- a/solution.py
+++ b/solution.py
@@ -59,52 +59,146 @@
     return m
 
 
-def build_schedule():
+def row_of(k):
+    kind = k[0]
+    if kind == "Bz":
+        return 0
+    if kind in ("Ay", "By"):
+        return -k[2]
+    return k[4] if kind == "Az" else 2
+
+
+SLOWER = 1.12
+LATENCY = 2.4
+AHEAD = (1.5, 0.8)
+GATE_FROM = 4.0
+RELS = (0, -1, 1, 2)
+
+
+def build_messages():
     msgs = {}
     for d in (1, -1):
-        msgs["X2", d] = (("x", d), 10.5, [])
-        msgs["X1", d] = (("x", d), 21.0, [])
-        msgs["X2f", d] = (("x", d), 10.5, [("X2", d)])
+        msgs["X2", d] = (("x", d), 8.8, [])
+        msgs["X1", d] = (("x", d), 17.6, [])
+        msgs["X2f", d] = (("x", d), 8.8, [("X2", d)])
     for h in (0, 1):
         msgs.update(half_messages(h))
+    return msgs
+
+
+def build_pieces():
+    p = {}
+
+    def add(name, cost, after=(), rows=(), sends=(), delay=0.0):
+        p[name] = (cost, list(after), list(rows), list(sends), delay)
+
+    z_swap = [(("z", 1), 2.5), (("z", -1), 2.5)]
+    y_swap = [(("y", 1), 0.9), (("y", -1), 0.9)]
+    add(("carry4",), 0.5, [("carry3",)])
+    add(("carry3",), 0.5, [("carry2",), ("dec_recv",)], (), z_swap, 2.5)
+    add(("carry2",), 0.4, [("carry1",), ("dec_recv",)], (), y_swap, 2.6)
+    add(("carry1",), 0.1, [("update",)], (), z_swap, 2.5)
+    convs = [("conv", rel) for rel in RELS]
+    add(("update",), 0.5, convs + [("delta",), ("state_conv",)])
+    ready = [("transpose", i) for i in range(5)]
+    for rel in RELS:
+        add(("conv", rel), 0.6, [("inner", rel, 0), ("inner", rel, 1), ("gains",)])
+        add(("inner", rel, 0), 0.9, ready, [(0, rel)])
+        add(("inner", rel, 1), 0.65, ready, [(0, rel)])
+    for i in range(4):
+        add(("norm", i), 0.56)
+    add(("halo",), 0.3, [("norm", 3)], (), (), 0.0)
+    for i in range(5):
+        add(("transpose", i), 0.42, [("halo",)])
+    add(("gains",), 0.2, [("norm", 3)])
+    for i in range(4):
+        add(("state_weight", i), 0.48, ready)
+    for i in range(3):
+        add(("state", i), 0.6, [("state_weight", e) for e in range(4)])
+    add(("state_conv",), 0.4, [("state", i) for i in range(3)])
+    add(("delta",), 1.2, ready + [("gains",)])
+    add(("scores",), 0.3, [("state_conv",)])
+    add(("dec_send",), 0.1, [("delta",)], (), (), 5.0)
+    for i in range(HEADS):
+        add(("mix", i), 0.16, [("delta",), ("scores",)])
+    add(("dec_recv",), 0.2, [("dec_send",)], (), (), 3.5)
+    mixes = [("mix", i) for i in range(HEADS)]
+    for rel in RELS:
+        add(("gated", rel), 0.12, [("inter", rel), ("gate", rel, 0), ("gate", rel, 1)])
+        add(("inter", rel), 0.2, [("carry4",), ("intra", 0), ("intra", 1)])
+    for i in range(2):
+        add(("intra", i), 0.9, mixes + convs)
+    for rel in RELS:
+        add(("gate", rel, 0), 0.53, ready, [(1, rel)])
+        add(("gate", rel, 1), 0.53, ready, [(1, rel)])
+    return p
+
+
+def build_program():
+    msgs, pieces = build_messages(), build_pieces()
     order = {k: i for i, k in enumerate(msgs)}
 
     def rank(k):
-        h = k[1] if k[0][0] in "AB" else 0
-        fan = 0 if k[0] in ("Bz", "Ay", "X2", "X2f") else 1
-        return (h, fan, order[k])
-
-    latency = 2.2
-    arrived, started = {}, {}
-    free = {}
-    pending = set(msgs)
-    while pending:
-        best = None
-        for k in pending:
-            link, dur, deps = msgs[k]
-            if any(q not in arrived for q in deps):
+        if k[0][0] == "X":
+            return (0, 9 if k[0] == "X1" else 0, order[k])
+        if k[0] in ("Bz", "Ay"):
+            p = 0
+        elif k[0] == "Ay2":
+            p = 0.5
+        elif k[0] == "Az":
+            p = 1 + k[3] + (0, 0.2, 0.4)[abs(k[4])]
+        else:
+            p = 1 + abs(k[3]) + (2 if k[0] == "By2" else 0)
+        return (k[1], p, order[k])
+
+    arrived, done, free, program = {}, {}, {}, []
+    todo = sorted(msgs, key=rank)
+    work = list(pieces)
+    now = 0.0
+    rows = {}
+    for k in msgs:
+        if k[0][0] in "AB":
+            rows.setdefault((k[1], row_of(k)), []).append(k)
+    while todo or work:
+        moved = True
+        while moved:
+            moved = False
+            for k in todo:
+                link, dur, deps = msgs[k]
+                later = k[0][0] != "X" and k[1] == 1
+                if free.get(link, 0.0) > now + AHEAD[later] or (later and now < GATE_FROM):
+                    continue
+                if any(arrived.get(q, 1e9) > now for q in deps):
+                    continue
+                start = max(now, free.get(link, 0.0))
+                free[link] = start + dur * SLOWER
+                arrived[k] = free[link] + LATENCY
+                program.append(("issue", k))
+                todo.remove(k)
+                now += 0.02
+                moved = True
+                break
+        for name in work:
+            cost, after, need, sends, delay = pieces[name]
+            if any(done.get(q, 1e9) > now for q in after):
                 continue
-            ready = max([arrived[q] for q in deps], default=0.0)
-            t = max(ready, free.get(link, 0.0))
-            key = (t, rank(k))
-            if best is None or key < best[0]:
-                best = (key, k, t)
-        _, k, t = best
-        link, dur, _ = msgs[k]
-        started[k] = t
-        free[link] = t + dur
-        arrived[k] = t + dur + latency
-        pending.remove(k)
-    events = []
-    for k in msgs:
-        ready = max([arrived[q] for q in msgs[k][2]], default=0.0)
-        events.append((max(ready, started[k] - 3.0), started[k], order[k], k))
-    events.sort()
-    half_done = [max(arrived[k] for k in msgs if k[0][0] in "AB" and k[1] == h) for h in (0, 1)]
-    return msgs, [(e[0], e[3]) for e in events], half_done
-
-
-MSGS, EVENTS, HALF_DONE = build_schedule()
+            if any(arrived.get(k, 1e9) > now for e in need for k in rows[e]):
+                continue
+            program.append(("piece", name))
+            work.remove(name)
+            now += cost
+            end = now
+            for link, dur in sends:
+                free[link] = max(now, free.get(link, 0.0)) + dur * SLOWER
+                end = max(end, free[link])
+            done[name] = end + delay
+            break
+        else:
+            now += 0.05
+    return msgs, program, done, arrived
+
+
+MSGS, PROGRAM, DONE, ARRIVED = build_program()
 IDS = {k: i for i, k in enumerate(MSGS)}
 N_MSG = len(MSGS)
 
@@ -114,7 +208,7 @@
     out,
     tok, own_a, own_b, own_f, sw, swd, cwin, og, wa, wb, nrm, nt, spf, cb, ct, dec, cum, ecum, tailw, d01, scores, mix, term, colt,
     p0s, p1s, inn, gat, vt, vw, u, yv, cs, cr, co, ci, tt, rowd, prefix,
-    sbf, scb, wr, relay, sq, rs_out, rs_in1, rs2_out, rs2_in, own_p,
+    sbf, scb, wr, relay, sq, rs_out, rs_in1, rs2_out, rs2_in, keep, own_p,
     halo, send, recv, xsend, xrecv, lsem,
 ):
     seq = lax.axis_index("seq")
@@ -226,23 +320,19 @@
         return remote(src, dst, send.at[i], recv.at[i], to)
 
     waited = set()
-    queue = list(EVENTS)
-
     def take(k):
         if k not in waited:
             waited.add(k)
             message(k).wait_recv()
 
-    def progress(until):
-        while queue and queue[0][0] <= until:
-            _, k = queue.pop(0)
-            for q in MSGS[k][2]:
-                take(q)
-            message(k).start()
-
-    def complete(h):
+    def issue(k):
+        for q in MSGS[k][2]:
+            take(q)
+        message(k).start()
+
+    def complete(h, rel):
         for k in MSGS:
-            if k[0][0] in "AB" and k[1] == h:
+            if k[0][0] in "AB" and k[1] == h and row_of(k) == rel:
                 take(k)
 
     extra_sends = []
@@ -268,7 +358,7 @@
             nrm[pl.ds(128 + r, 16), :] = norm_rows(tok[pl.ds(r, 16), :]).astype(BF)
             return carry
 
-        lax.fori_loop(0, 8, step, 0)
+        lax.fori_loop(0, 8, step, 0, unroll=2)
 
     def piece_halo():
         halo_copy.wait_recv()
@@ -283,19 +373,20 @@
             ].T
             return carry
 
-        lax.fori_loop(0, D // 128, step, 0)
-
-    def piece_state_weight():
-        sw_copy.wait()
+        lax.fori_loop(0, D // 128, step, 0, unroll=5)
+
+    def piece_state_weight(part):
+        if part == 0:
+            sw_copy.wait()
 
         def step(i, carry):
-            r = pl.multiple_of(i * 128, 128)
+            r = pl.multiple_of(i * 128 + part * 640, 128)
             v = sw[pl.ds(r, 128), :, :].astype(F32)
             swd[pl.ds(r, 128), 0:128] = v[:, 0, :].astype(BF)
             swd[pl.ds(r, 128), 128:256] = v[:, 1, :].astype(BF)
             return carry
 
-        lax.fori_loop(0, D // 128, step, 0)
+        lax.fori_loop(0, 5, step, 0)
 
     def piece_state(part):
         r = part * 176
@@ -345,6 +436,8 @@
         term[0:HEADS, :] = jnp.log(delta) - run
         for q in range(4):
             colt[q * 128 : (q + 1) * 128, :] = term[:, q * 128 : (q + 1) * 128].T
+
+    def piece_scores():
         for b in range(2):
             s = slice(b * SPAN, (b + 1) * SPAN)
             scores[b] = dot(cb[s, :], ct[:, s])
@@ -385,24 +478,26 @@
                         arg = jnp.where(keep, arg, -jnp.inf)
                     mix[(h, b) + sl] = (scores[(b,) + sl] * jnp.exp(arg)).astype(BF)
 
-    def product(h, r, first, width):
+    def product(h, r, first, cols):
         la = wa[h, r].reshape(NZ * 40, KA)
         lb = wb[h, r].reshape(NZ * 40, KB)
-        cols = slice(first, first + width)
-        p0s[:, :width] = dot(la, nt[0:512, cols]) + dot(lb, nt[512:1280, cols])
-        p1s[:, :width] = dot(la, nt[1280:1792, cols]) + dot(lb, nt[1792:2560, cols])
-
-    def piece_inner(r):
-        product(0, r, 0, 640)
+        n = slice(first + cols.start, first + cols.stop)
+        p0s[:, cols] = dot(la, nt[0:512, n]) + dot(lb, nt[512:1280, n])
+        p1s[:, cols] = dot(la, nt[1280:1792, n]) + dot(lb, nt[1792:2560, n])
+
+    def piece_inner(r, part):
+        cols = (slice(0, 384), slice(384, 640))[part]
+        product(0, r, 0, cols)
         for i in range(NZ):
-            v = p0s[40 * i : 40 * i + 20, :] + p1s[40 * i + 20 : 40 * i + 40, :]
-            inn[r, 20 * i : 20 * i + 20, :] = v.astype(BF).astype(F32)
-
-    def piece_gate(r):
-        product(1, r, 128, 512)
+            v = p0s[40 * i : 40 * i + 20, cols] + p1s[40 * i + 20 : 40 * i + 40, cols]
+            inn[r, 20 * i : 20 * i + 20, cols] = v.astype(BF).astype(F32)
+
+    def piece_gate(r, part):
+        cols = slice(part * SPAN, (part + 1) * SPAN)
+        product(1, r, 128, cols)
         for i in range(NZ):
-            v = p0s[40 * i : 40 * i + 20, :512] + p1s[40 * i + 20 : 40 * i + 40, :512]
-            gat[r, 20 * i : 20 * i + 20, :] = v.astype(BF).astype(F32)
+            v = p0s[40 * i : 40 * i + 20, cols] + p1s[40 * i + 20 : 40 * i + 40, cols]
+            gat[r, 20 * i : 20 * i + 20, cols] = v.astype(BF).astype(F32)
 
     def piece_conv(r):
         def step(i, carry):
@@ -416,7 +511,7 @@
             vt[pl.ds(row, 32), :] = (acc * lax.logistic(acc)).astype(BF)
             return carry
 
-        lax.fori_loop(0, 5, step, 0)
+        lax.fori_loop(0, 5, step, 0, unroll=5)
 
     def head_rows(h):
         return pl.ds(pl.multiple_of(h * 64, 64), 64)
@@ -426,7 +521,7 @@
             vw[head_rows(h), :] = (vt[head_rows(h), :].astype(F32) * tailw[pl.ds(h, 1), :]).astype(BF)
             return carry
 
-        lax.fori_loop(0, HEADS, weigh, 0)
+        lax.fori_loop(0, HEADS, weigh, 0, unroll=2)
         for b in range(2):
             s = slice(b * SPAN, (b + 1) * SPAN)
             u[b] = dot(vw[:, s], cb[s, :])
@@ -437,7 +532,7 @@
                 cs[j, h] = v[8 * j : 8 * j + 8, :].astype(BF)
             return carry
 
-        lax.fori_loop(0, HEADS, total, 0)
+        lax.fori_loop(0, HEADS, total, 0, unroll=2)
         cr[z] = cs[z]
 
     carry1, carry2, carry3 = [], [], []
@@ -453,8 +548,8 @@
         for k in range(NZ):
             prefix[k] = run
             run = run * dec[k] + cr[k].astype(F32)
-        tt[4] = run
-        tt[y] = run
+        tt[4] = run.astype(BF)
+        tt[y] = run.astype(BF)
         for k in range(1, NY):
             carry2.append(extra(tt.at[4], tt.at[y], dev(dy=k), 17 + k))
 
@@ -463,7 +558,7 @@
             q.wait_recv()
         r = jnp.zeros((HEADS, 8, 128), F32)
         for k in range(NY - 1):
-            r = jnp.where(y > k, r * rowd[k] + tt[k], r)
+            r = jnp.where(y > k, r * rowd[k] + tt[k].astype(F32), r)
         for k in range(NZ):
             co[k] = (prefix[k] + r).astype(BF)
             r = r * dec[k]
@@ -491,45 +586,46 @@
             yv[head_rows(h), s] = dot(v, mix[h, b]) + skip[h] * v.astype(F32)
             return carry
 
-        lax.fori_loop(0, HEADS, step, 0)
-
-    def piece_inter(b):
-        s = slice(b * SPAN, (b + 1) * SPAN)
-
-        def step(h, carry):
-            got = dot(sbf[b, head_rows(h), :], ct[:, s])
-            yv[head_rows(h), s] = yv[head_rows(h), s] + ecum[pl.ds(h, 1), s] * got
+        lax.fori_loop(0, HEADS, step, 0, unroll=2)
+
+    def piece_inter(r):
+        rows = pl.ds(pl.multiple_of(r * 160, 160), 160)
+        for b in range(2):
+            s = slice(b * SPAN, (b + 1) * SPAN)
+            p0s[0:160, s] = dot(sbf[b, rows, :], ct[:, s])
+
+        def step(i, carry):
+            q = pl.multiple_of(i * 32, 32)
+            row = pl.ds(pl.multiple_of(r * 160 + q, 32), 32)
+            e = ecum[pl.ds((5 * r + i) // 2, 1), :]
+            yv[row, :] = yv[row, :] + e * p0s[pl.ds(q, 32), 0:TOK]
             return carry
 
-        lax.fori_loop(0, HEADS, step, 0)
+        lax.fori_loop(0, 5, step, 0, unroll=5)
 
     pair_copies, sq_copies = [], []
-
-    def piece_gated(b):
-        s = slice(b * SPAN, (b + 1) * SPAN)
-        total = jnp.zeros((8, SPAN), F32)
-        for r in range(NY):
-
-            def step(i, total):
-                q = pl.multiple_of(i * 32, 32)
-                row = pl.multiple_of(r * 160 + q, 32)
-                g = gat[r, pl.ds(q, 32), s]
-                v = yv[pl.ds(row, 32), s] * (g * lax.logistic(g))
-                for e in range(4):
-                    w = v[8 * e : 8 * e + 8, :]
-                    total = total + w * w
-                scb[c, pl.ds(row, 32), s] = (v * og[pl.ds(row, 32), 0:1]).astype(BF)
-                return total
-
-            total = lax.fori_loop(0, 5, step, total)
-        sq[8, :, s] = total
-        own = scb.at[c, :, pl.ds(b * SPAN, SPAN)]
-        pair_copies.append(extra(own, own, dev(dc=1), 28 + b))
+    sq[8] = jnp.zeros((8, TOK), F32)
+
+    def piece_gated(r, slot):
+        def step(i, total):
+            q = pl.multiple_of(i * 32, 32)
+            row = pl.ds(pl.multiple_of(r * 160 + q, 32), 32)
+            g = gat[r, pl.ds(q, 32), :]
+            v = yv[row, :] * (g * lax.logistic(g))
+            for e in range(4):
+                w = v[8 * e : 8 * e + 8, :]
+                total = total + w * w
+            scb[c, row, :] = (v * og[row, 0:1]).astype(BF)
+            return total
+
+        sq[8] = lax.fori_loop(0, 5, step, sq[8], unroll=5)
+        own = scb.at[c, pl.ds(pl.multiple_of(r * 160, 160), 160)]
+        pair_copies.append(extra(own, own, dev(dc=1), 28 + slot))
 
     def piece_squares():
         sq[grp] = sq[8]
         for k in range(1, 8):
-            sq_copies.append(extra(sq.at[8], sq.at[grp], dev(dx=k // 2, dc=k % 2), 29 + k))
+            sq_copies.append(extra(sq.at[8], sq.at[grp], dev(dx=k // 2, dc=k % 2), 31 + k))
 
     def project(dx, half):
         s = slice(half * SPAN, (half + 1) * SPAN)
@@ -544,61 +640,49 @@
             cwin[cols, :] = term[:, 0:128].T
             og[cols, :] = jnp.broadcast_to(og_in[cols].reshape(1, 128), (128, 128)).T
 
-    def piece_name(piece):
-        inside = getattr(piece, "func", piece)
-        return inside.__name__ + "".join(f"#i={a}" for a in getattr(piece, "args", ()))
-
     def call(piece, *args):
-        with jax.named_scope(piece.__name__ + "".join(f"#i={a}" for a in args)):
+        with jax.named_scope(piece.__name__ + "".join(f"#i={a}" for a in args if isinstance(a, int))):
             return piece(*args)
 
-    clock = 0.5
-    progress(clock)
-    front = [(functools.partial(piece_norm, i), 0.5) for i in range(4)]
-    front += [(piece_halo, 0.1), (piece_gains, 0.4)]
-    front += [(functools.partial(piece_transpose, i), 0.5) for i in range(5)]
-    front += [(piece_state_weight, 1.0)]
-    front += [(functools.partial(piece_state, i), 0.3) for i in range(3)]
-    front += [(piece_state_conv, 0.3), (piece_delta, 0.6), (piece_dec_send, 0.1)]
-    front += [(functools.partial(piece_mix, i), 0.25) for i in range(HEADS)]
-    front += [(piece_dec_recv, 0.1)]
-    for piece, cost in front:
-        with jax.named_scope(piece_name(piece)):
-            piece()
-        clock += cost
-        progress(clock)
-    progress(HALF_DONE[0])
-    clock = HALF_DONE[0]
-    call(complete, 0)
-    middle = []
-    for i in range(NY):
-        middle += [(functools.partial(piece_inner, i), 1.0), (functools.partial(piece_conv, i), 0.4)]
-    middle += [(piece_update, 0.6), (piece_carry1, 0.1)]
-    middle += [(functools.partial(piece_intra, i), 0.8) for i in range(2)]
-    for piece, cost in middle:
-        with jax.named_scope(piece_name(piece)):
-            piece()
-        clock += cost
-        progress(clock)
-    clock += 3.0
-    progress(clock)
-    call(piece_carry2)
-    clock += 4.0
-    progress(clock)
-    call(piece_carry3)
-    clock += 5.0
-    progress(clock)
-    call(piece_carry4)
-    for i in range(2):
-        call(piece_inter, i)
-        clock += 0.4
-        progress(clock)
-    progress(1e9)
-    call(complete, 1)
-    for i in range(NY):
-        call(piece_gate, i)
-    for i in range(2):
-        call(piece_gated, i)
+    def inner_row(rel, part):
+        complete(0, rel)
+        piece_inner(yy(rel), part)
+
+    def gate_row(rel, part):
+        complete(1, rel)
+        piece_gate(yy(rel), part)
+
+    does = {
+        "norm": piece_norm,
+        "halo": piece_halo,
+        "gains": piece_gains,
+        "transpose": piece_transpose,
+        "state_weight": piece_state_weight,
+        "state": piece_state,
+        "state_conv": piece_state_conv,
+        "delta": piece_delta,
+        "scores": piece_scores,
+        "dec_send": piece_dec_send,
+        "dec_recv": piece_dec_recv,
+        "mix": piece_mix,
+        "inner": inner_row,
+        "conv": lambda rel: piece_conv(yy(rel)),
+        "update": piece_update,
+        "carry1": piece_carry1,
+        "carry2": piece_carry2,
+        "carry3": piece_carry3,
+        "carry4": piece_carry4,
+        "intra": piece_intra,
+        "inter": lambda rel: piece_inter(yy(rel)),
+        "gate": gate_row,
+        "gated": lambda rel: piece_gated(yy(rel), rel + 1),
+    }
+    for what, k in PROGRAM:
+        if what == "issue":
+            issue(k)
+        else:
+            with jax.named_scope("#".join(str(e) for e in k)):
+                does[k[0]](*k[1:])
     call(piece_squares)
     with jax.named_scope("wait_weights"):
         own_out.wait()
@@ -607,35 +691,58 @@
     with jax.named_scope("wait_pair"):
         for q in pair_copies:
             q.wait_recv()
-    far = []
-    for half, d in ((0, 1), (1, -1)):
-        rs_out[half] = call(project, 2, half).astype(BF)
-        far.append(extra(rs_out.at[half], rs_in1.at[half], dev(dx=d), 40 + half))
-    near = []
-    for i, d in enumerate((1, -1)):
-        direct = 1 if d == 1 else 0
-        rs2_out[i, direct] = call(project, d, direct).astype(BF)
-        near.append(extra(rs2_out.at[i, direct], rs2_in.at[i, direct], dev(dx=d), 42 + 2 * i))
-    for i, d in enumerate((1, -1)):
-        relayed = 0 if d == 1 else 1
-        v = call(project, d, relayed)
-        with jax.named_scope("wait_far"):
-            far[relayed].wait_recv()
-        rs2_out[i, relayed] = (v + rs_in1[relayed].astype(F32)).astype(BF)
-        near.append(extra(rs2_out.at[i, relayed], rs2_in.at[i, relayed], dev(dx=d), 43 + 2 * i))
-    for half in range(2):
-        own_p[half] = call(project, 0, half)
-    for q in sq_copies:
-        q.wait_recv()
+
+    top, low = slice(0, 160), slice(160, 320)
+    far, near = {}, []
+
+    def send_far(half):
+        got = call(project, 2, half)
+        rs_out[half] = got.astype(BF)
+        for i, d in enumerate((1, -1)):
+            rows = pl.ds(160 * i, 160)
+            far[half, d] = extra(
+                rs_out.at[half, rows], rs_in1.at[half, rows], dev(dx=d), 40 + 2 * half + i
+            )
+
+    def send_direct(half):
+        for i, d in enumerate((1, -1)):
+            keep[i] = call(project, d, half)
+            rows = low if d == 1 else top
+            rs2_out[i, half, rows] = keep[i, rows].astype(BF)
+            rows = pl.ds(160 * (1 - i), 160)
+            part = (i, half, rows)
+            near.append(extra(rs2_out.at[part], rs2_in.at[part], dev(dx=d), 44 + 4 * half + i))
+
+    def send_relayed(half):
+        for i, d in enumerate((1, -1)):
+            with jax.named_scope("wait_far"):
+                far[half, d].wait_recv()
+            rows = top if d == 1 else low
+            rs2_out[i, half, rows] = (keep[i, rows] + rs_in1[half, rows].astype(F32)).astype(BF)
+            rows = pl.ds(160 * i, 160)
+            part = (i, half, rows)
+            near.append(extra(rs2_out.at[part], rs2_in.at[part], dev(dx=d), 46 + 4 * half + i))
+
+    send_far(0)
+    send_direct(0)
+    send_far(1)
+    send_relayed(0)
+    send_direct(1)
+    own_p[0] = call(project, 0, 0)
+    send_relayed(1)
+    own_p[1] = call(project, 0, 1)
+    with jax.named_scope("wait_sq"):
+        for q in sq_copies:
+            q.wait_recv()
     total = sq[0]
     for k in range(1, 8):
         total = total + sq[k]
     total = jnp.sum(total, axis=0, keepdims=True)
     scale = lax.rsqrt(total / (8 * CH) + EPS)
-    with jax.named_scope("wait_near"):
-        for q in near:
-            q.wait_recv()
     for half in range(2):
+        with jax.named_scope("wait_near"):
+            for q in near[4 * half : 4 * half + 4]:
+                q.wait_recv()
         v = own_p[half] + rs2_in[0, half].astype(F32) + rs2_in[1, half].astype(F32)
         s = slice(half * SPAN, (half + 1) * SPAN)
         out[:, s] = (v * scale[:, s]).astype(BF)
@@ -691,7 +798,7 @@
         V((NZ, HEADS, 8, 128), BF),
         V((NZ, HEADS, 8, 128), BF),
         V((NZ, HEADS, 8, 128), BF),
-        V((5, HEADS, 8, 128), F32),
+        V((5, HEADS, 8, 128), BF),
         V((5, HEADS, 1, 128), F32),
         V((NZ, HEADS, 8, 128), F32),
         V((2, CH, 128), BF),
@@ -704,11 +811,12 @@
         V((2, 2, FEAT, SPAN), BF),
         V((2, 2, FEAT, SPAN), BF),
         V((2, FEAT, SPAN), F32),
+        V((2, FEAT, SPAN), F32),
         V((16, D), BF),
         pltpu.SemaphoreType.DMA((N_MSG,)),
         pltpu.SemaphoreType.DMA((N_MSG,)),
-        pltpu.SemaphoreType.DMA((48,)),
-        pltpu.SemaphoreType.DMA((48,)),
+        pltpu.SemaphoreType.DMA((52,)),
+        pltpu.SemaphoreType.DMA((52,)),
         pltpu.SemaphoreType.DMA((6,)),
     ]
     return pl.pallas_call(

time: 105 us -> 84.8 us (0.81)
  Pallas kernels: 103 us -> 83 us
    pallas_call x1, Pallas kernels: 103 us -> 83 us  [run(): pl.pallas_call(kernel, out_shape=jax.ShapeDtypeStruct((FEAT, TOK), BF), i...]
where the time goes in v3:
time: 84.8 us; the launch traced here: 84.7 us
  Pallas kernels  83 us (98%)
  local copies, waits for them, and re-layouts  1.72 us (2%)
    pallas_call x1, Pallas kernels, run(): pl.pallas_call(kernel, out_shape=jax.ShapeDtypeStruct((FEAT, TOK), BF), i...  83 us
    unnamed x1, local copies, waits for them, and re-layouts  1.72 us

profile of v3, /device:TPU:1, one launch (start us, length us, event | category | flops | bytes accessed | tf_op | source)
XLA Modules:
  0.0 84.7 jit_solution(16195469694859288376)
XLA Ops:
  0.0 83.0 %layer.1 = bf16[320,512]{1,0:T(8,128)(2,1)} custom-call(bf16[512,2560]{1,0:T(8,128)(2,1)} %tok_in.1, f32[2560]{0:T(1024)} %gain.1, bf16[20,2,2560]{2,1,0:T(2,128)(2,1)} %bitcast.6, bf16[2560,2,128]{2,1,0:T(2,128)(2,1)} %sw_in.1, bf16[10,2560]{1,0:T(8,128)(2,1)} %bitcast.7, f32[10]{0:T(128)} %bias.1, f32[10]{0:T(128)} %rate.1, f32[10]{0:T(128)} %skip.1, ...), custom_call_target="tpu_custom_call" | custom-call | tf_op jit(solution)/shard_map/layer/pallas_call | solution.py:822
  83.0 1.7 %copy.14 = bf16[512,320]{0,1:T(8,128)(2,1)} copy(bf16[512,320]{0,1:T(8,128)(2,1)} %bitcast.5) | data formatting | bytes 655360

commit v4 on v3

--- a/solution.py
+++ b/solution.py
@@ -73,6 +73,7 @@
 AHEAD = (1.5, 0.8)
 GATE_FROM = 4.0
 RELS = (0, -1, 1, 2)
+FAR_FIRST = (4, 3, 5, 2, 6, 1, 7)
 
 
 def build_messages():
@@ -102,9 +103,9 @@
     add(("update",), 0.5, convs + [("delta",), ("state_conv",)])
     ready = [("transpose", i) for i in range(5)]
     for rel in RELS:
-        add(("conv", rel), 0.6, [("inner", rel, 0), ("inner", rel, 1), ("gains",)])
-        add(("inner", rel, 0), 0.9, ready, [(0, rel)])
-        add(("inner", rel, 1), 0.65, ready, [(0, rel)])
+        add(("conv", rel), 1.0, [("mul", 0, rel, "A"), ("mul", 0, rel, "B"), ("gains",)])
+        add(("mul", 0, rel, "A"), 0.6, ready, [(0, rel, "A")])
+        add(("mul", 0, rel, "B"), 0.85, ready, [(0, rel, "B")])
     for i in range(4):
         add(("norm", i), 0.56)
     add(("halo",), 0.3, [("norm", 3)], (), (), 0.0)
@@ -124,13 +125,14 @@
     add(("dec_recv",), 0.2, [("dec_send",)], (), (), 3.5)
     mixes = [("mix", i) for i in range(HEADS)]
     for rel in RELS:
-        add(("gated", rel), 0.12, [("inter", rel), ("gate", rel, 0), ("gate", rel, 1)])
+        add(("gated", rel), 0.12, [("inter", rel), ("gate", rel)])
+        add(("gate", rel), 0.35, [("mul", 1, rel, "A"), ("mul", 1, rel, "B")])
         add(("inter", rel), 0.2, [("carry4",), ("intra", 0), ("intra", 1)])
     for i in range(2):
         add(("intra", i), 0.9, mixes + convs)
     for rel in RELS:
-        add(("gate", rel, 0), 0.53, ready, [(1, rel)])
-        add(("gate", rel, 1), 0.53, ready, [(1, rel)])
+        add(("mul", 1, rel, "A"), 0.5, [("conv", rel)], [(1, rel, "A")])
+        add(("mul", 1, rel, "B"), 0.7, [("conv", rel)], [(1, rel, "B")])
     return p
 
 
@@ -158,7 +160,7 @@
     rows = {}
     for k in msgs:
         if k[0][0] in "AB":
-            rows.setdefault((k[1], row_of(k)), []).append(k)
+            rows.setdefault((k[1], row_of(k), k[0][0]), []).append(k)
     while todo or work:
         moved = True
         while moved:
@@ -204,10 +206,11 @@
 
 
 def kernel(
-    tok_in, gain, own_in, sw_in, st, bias, rate, skip, cw_in, cwst, og_in, ow,
+    tok_in, gain_in, own_w, sw_in, st_in, bias_in, rate_in, skip_in, cw_w, cwst_in, og_w, ow,
     out,
+    gain, own_in, st, bias, rate, skip, cw_in, cwst, og_in,
     tok, own_a, own_b, own_f, sw, swd, cwin, og, wa, wb, nrm, nt, spf, cb, ct, dec, cum, ecum, tailw, d01, scores, mix, term, colt,
-    p0s, p1s, inn, gat, vt, vw, u, yv, cs, cr, co, ci, tt, rowd, prefix,
+    acc, joined, inn, gat, vt, vw, u, yv, cs, cr, co, ci, tt, rowd, prefix,
     sbf, scb, wr, relay, sq, rs_out, rs_in1, rs2_out, rs2_in, keep, own_p,
     halo, send, recv, xsend, xrecv, lsem,
 ):
@@ -242,6 +245,13 @@
     def feature_columns(d, first, count):
         return ow.at[:, pl.ds(pl.multiple_of(xx(d) * 1280 + first, 128), count)]
 
+    own_copy = pltpu.make_async_copy(own_w, own_in, lsem.at[6])
+    own_copy.start()
+    small = ((gain_in, gain), (st_in, st), (bias_in, bias), (rate_in, rate), (skip_in, skip),
+             (cw_w, cw_in), (cwst_in, cwst), (og_w, og_in))
+    small_copies = [pltpu.make_async_copy(a, b, lsem.at[7 + i]) for i, (a, b) in enumerate(small)]
+    for q in small_copies:
+        q.start()
     tok_copies = []
     for q in range(4):
         part = pl.ds(q * 128, 128)
@@ -251,6 +261,7 @@
     sw_copy.start()
     own_out = pltpu.make_async_copy(feature_columns(0, 0, 1280), wr.at[x], lsem.at[5])
     own_out.start()
+    own_copy.wait()
     for r in range(20):
         v = own_in[r].astype(F32)
         for h in (0, 1):
@@ -265,6 +276,8 @@
         wa[h, y, z] = v[:, :KA]
         wb[h, y, z] = v[:, KA:]
     nrm[0:128, :] = jnp.zeros((128, D), BF)
+    for q in small_copies:
+        q.wait()
     with jax.named_scope("barrier"):
         pl.semaphore_wait(barrier, len(peers))
 
@@ -330,9 +343,9 @@
             take(q)
         message(k).start()
 
-    def complete(h, rel):
+    def complete(h, rel, route):
         for k in MSGS:
-            if k[0][0] in "AB" and k[1] == h and row_of(k) == rel:
+            if k[0][0] == route and k[1] == h and row_of(k) == rel:
                 take(k)
 
     extra_sends = []
@@ -478,26 +491,27 @@
                         arg = jnp.where(keep, arg, -jnp.inf)
                     mix[(h, b) + sl] = (scores[(b,) + sl] * jnp.exp(arg)).astype(BF)
 
-    def product(h, r, first, cols):
-        la = wa[h, r].reshape(NZ * 40, KA)
-        lb = wb[h, r].reshape(NZ * 40, KB)
-        n = slice(first + cols.start, first + cols.stop)
-        p0s[:, cols] = dot(la, nt[0:512, n]) + dot(lb, nt[512:1280, n])
-        p1s[:, cols] = dot(la, nt[1280:1792, n]) + dot(lb, nt[1792:2560, n])
-
-    def piece_inner(r, part):
-        cols = (slice(0, 384), slice(384, 640))[part]
-        product(0, r, 0, cols)
-        for i in range(NZ):
-            v = p0s[40 * i : 40 * i + 20, cols] + p1s[40 * i + 20 : 40 * i + 40, cols]
-            inn[r, 20 * i : 20 * i + 20, cols] = v.astype(BF).astype(F32)
-
-    def piece_gate(r, part):
-        cols = slice(part * SPAN, (part + 1) * SPAN)
-        product(1, r, 128, cols)
-        for i in range(NZ):
-            v = p0s[40 * i : 40 * i + 20, cols] + p1s[40 * i + 20 : 40 * i + 40, cols]
-            gat[r, 20 * i : 20 * i + 20, cols] = v.astype(BF).astype(F32)
+    begun = set()
+
+    def piece_mul(h, rel, route):
+        i = RELS.index(rel)
+        held, k0, kn = (wa, 0, KA) if route == "A" else (wb, KA, KB)
+        lhs = held[h, yy(rel)].reshape(NZ * 40, kn)
+        for cols in (slice(0, 256), slice(256, 512), slice(512, 640))[: 3 - h]:
+            n = slice(128 * h + cols.start, 128 * h + cols.stop)
+            for e in (0, 1):
+                v = dot(lhs, nt[1280 * e + k0 : 1280 * e + k0 + kn, n])
+                if (h, rel) in begun:
+                    acc[i, e, :, cols] += v
+                else:
+                    acc[i, e, :, cols] = v
+        begun.add((h, rel))
+
+    def unfold(rel, into, width):
+        i, r = RELS.index(rel), yy(rel)
+        for e in range(NZ):
+            v = acc[i, 0, 40 * e : 40 * e + 20, :width] + acc[i, 1, 40 * e + 20 : 40 * e + 40, :width]
+            into[r, 20 * e : 20 * e + 20, :] = v.astype(BF).astype(F32)
 
     def piece_conv(r):
         def step(i, carry):
@@ -538,7 +552,7 @@
     carry1, carry2, carry3 = [], [], []
 
     def piece_carry1():
-        for k in range(1, NZ):
+        for k in FAR_FIRST:
             carry1.append(extra(cs.at[zz(k)], cr.at[z], dev(dz=k), 10 + k))
 
     def piece_carry2():
@@ -550,7 +564,7 @@
             run = run * dec[k] + cr[k].astype(F32)
         tt[4] = run.astype(BF)
         tt[y] = run.astype(BF)
-        for k in range(1, NY):
+        for k in (2, 1, 3):
             carry2.append(extra(tt.at[4], tt.at[y], dev(dy=k), 17 + k))
 
     def piece_carry3():
@@ -563,7 +577,7 @@
             co[k] = (prefix[k] + r).astype(BF)
             r = r * dec[k]
         ci[z] = co[z]
-        for k in range(1, NZ):
+        for k in FAR_FIRST:
             carry3.append(extra(co.at[zz(k)], ci.at[z], dev(dz=k), 20 + k))
 
     def piece_carry4():
@@ -592,13 +606,13 @@
         rows = pl.ds(pl.multiple_of(r * 160, 160), 160)
         for b in range(2):
             s = slice(b * SPAN, (b + 1) * SPAN)
-            p0s[0:160, s] = dot(sbf[b, rows, :], ct[:, s])
+            joined[:, s] = dot(sbf[b, rows, :], ct[:, s])
 
         def step(i, carry):
             q = pl.multiple_of(i * 32, 32)
             row = pl.ds(pl.multiple_of(r * 160 + q, 32), 32)
             e = ecum[pl.ds((5 * r + i) // 2, 1), :]
-            yv[row, :] = yv[row, :] + e * p0s[pl.ds(q, 32), 0:TOK]
+            yv[row, :] = yv[row, :] + e * joined[pl.ds(q, 32), :]
             return carry
 
         lax.fori_loop(0, 5, step, 0, unroll=5)
@@ -644,13 +658,13 @@
         with jax.named_scope(piece.__name__ + "".join(f"#i={a}" for a in args if isinstance(a, int))):
             return piece(*args)
 
-    def inner_row(rel, part):
-        complete(0, rel)
-        piece_inner(yy(rel), part)
-
-    def gate_row(rel, part):
-        complete(1, rel)
-        piece_gate(yy(rel), part)
+    def mul(h, rel, route):
+        complete(h, rel, route)
+        piece_mul(h, rel, route)
+
+    def conv(rel):
+        unfold(rel, inn, 640)
+        piece_conv(yy(rel))
 
     does = {
         "norm": piece_norm,
@@ -665,8 +679,8 @@
         "dec_send": piece_dec_send,
         "dec_recv": piece_dec_recv,
         "mix": piece_mix,
-        "inner": inner_row,
-        "conv": lambda rel: piece_conv(yy(rel)),
+        "mul": mul,
+        "conv": conv,
         "update": piece_update,
         "carry1": piece_carry1,
         "carry2": piece_carry2,
@@ -674,7 +688,7 @@
         "carry4": piece_carry4,
         "intra": piece_intra,
         "inter": lambda rel: piece_inter(yy(rel)),
-        "gate": gate_row,
+        "gate": lambda rel: unfold(rel, gat, TOK),
         "gated": lambda rel: piece_gated(yy(rel), rel + 1),
     }
     for what, k in PROGRAM:
@@ -755,13 +769,18 @@
 
 def run(*args):
     vm = pl.BlockSpec(memory_space=pltpu.VMEM)
-    specs = [vm] * 12
-    for i in (5, 6, 7):
-        specs[i] = pl.BlockSpec(memory_space=pltpu.SMEM)
-    for i in (0, 3, 11):
-        specs[i] = pl.BlockSpec(memory_space=pl.ANY)
+    specs = [pl.BlockSpec(memory_space=pl.ANY)] * 12
     V = pltpu.VMEM
     scratch = [
+        V((D,), F32),
+        V((20, 2, D), BF),
+        V((HEADS, D), BF),
+        pltpu.SMEM((HEADS,), F32),
+        pltpu.SMEM((HEADS,), F32),
+        pltpu.SMEM((HEADS,), F32),
+        V((4, CH), BF),
+        V((4, 2, 128), BF),
+        V((CH,), F32),
         V((TOK, D), BF),
         V((2, 40, KA), BF),
         V((2, 40, KB), BF),
@@ -786,8 +805,8 @@
         V((HEADS, 2, SPAN, SPAN), BF),
         V((128, TOK), F32),
         V((TOK, 128), F32),
-        V((320, 640), F32),
-        V((320, 640), F32),
+        V((4, 2, 320, 640), F32),
+        V((160, TOK), F32),
         V((NY, 160, 640), F32),
         V((NY, 160, TOK), F32),
         V((CH, TOK), BF),
@@ -817,7 +836,7 @@
         pltpu.SemaphoreType.DMA((N_MSG,)),
         pltpu.SemaphoreType.DMA((52,)),
         pltpu.SemaphoreType.DMA((52,)),
-        pltpu.SemaphoreType.DMA((6,)),
+        pltpu.SemaphoreType.DMA((15,)),
     ]
     return pl.pallas_call(
         kernel,

time: 84.8 us -> 82 us (0.967)
  Pallas kernels: 83 us -> 80.2 us
    pallas_call x1, Pallas kernels: 83 us -> 80.2 us  [run(): pl.pallas_call(kernel, out_shape=jax.ShapeDtypeStruct((FEAT, TOK), BF), i...]
where the time goes in v4:
time: 82 us; the launch traced here: 81.9 us
  Pallas kernels  80.2 us (98%)
  local copies, waits for them, and re-layouts  1.72 us (2%)
    pallas_call x1, Pallas kernels, run(): pl.pallas_call(kernel, out_shape=jax.ShapeDtypeStruct((FEAT, TOK), BF), i...  80.2 us
    unnamed x1, local copies, waits for them, and re-layouts  1.72 us

profile of v4, /device:TPU:1, one launch (start us, length us, event | category | flops | bytes accessed | tf_op | source)
XLA Modules:
  0.0 81.9 jit_solution(17436576471734724567)
XLA Ops:
  0.0 80.2 %layer.1 = bf16[320,512]{1,0:T(8,128)(2,1)} custom-call(bf16[512,2560]{1,0:T(8,128)(2,1)} %tok_in.1, f32[2560]{0:T(1024)} %gain_in.1, bf16[20,2,2560]{2,1,0:T(2,128)(2,1)} %bitcast.6, bf16[2560,2,128]{2,1,0:T(2,128)(2,1)} %sw_in.1, bf16[10,2560]{1,0:T(8,128)(2,1)} %bitcast.7, f32[10]{0:T(128)} %bias_in.1, f32[10]{0:T(128)} %rate_in.1, f32[10]{0:T(128)} %skip_in.1, ...), custom_call_target="tpu_custom_call" | custom-call | tf_op jit(solution)/shard_map/layer/pallas_call | solution.py:841
  80.2 1.7 %copy.14 = bf16[512,320]{0,1:T(8,128)(2,1)} copy(bf16[512,320]{0,1:T(8,128)(2,1)} %bitcast.5) | data formatting | bytes 655360

commit v5 on v4

--- a/solution.py
+++ b/solution.py
@@ -70,8 +70,8 @@
 
 SLOWER = 1.12
 LATENCY = 2.4
-AHEAD = (1.5, 0.8)
-GATE_FROM = 4.0
+AHEAD = (1.2, 0.3)
+GATE_FROM = 0.0
 RELS = (0, -1, 1, 2)
 FAR_FIRST = (4, 3, 5, 2, 6, 1, 7)
 
@@ -103,9 +103,9 @@
     add(("update",), 0.5, convs + [("delta",), ("state_conv",)])
     ready = [("transpose", i) for i in range(5)]
     for rel in RELS:
-        add(("conv", rel), 1.0, [("mul", 0, rel, "A"), ("mul", 0, rel, "B"), ("gains",)])
-        add(("mul", 0, rel, "A"), 0.6, ready, [(0, rel, "A")])
-        add(("mul", 0, rel, "B"), 0.85, ready, [(0, rel, "B")])
+        add(("conv", rel), 0.4, [("mul", 0, rel, "A"), ("mul", 0, rel, "B"), ("gains",)])
+        add(("mul", 0, rel, "A"), 0.44, ready, [(0, rel, "A")])
+        add(("mul", 0, rel, "B"), 0.58, ready, [(0, rel, "B")])
     for i in range(4):
         add(("norm", i), 0.56)
     add(("halo",), 0.3, [("norm", 3)], (), (), 0.0)
@@ -126,13 +126,13 @@
     mixes = [("mix", i) for i in range(HEADS)]
     for rel in RELS:
         add(("gated", rel), 0.12, [("inter", rel), ("gate", rel)])
-        add(("gate", rel), 0.35, [("mul", 1, rel, "A"), ("mul", 1, rel, "B")])
+        add(("gate", rel), 0.05, [("mul", 1, rel, "A"), ("mul", 1, rel, "B")])
         add(("inter", rel), 0.2, [("carry4",), ("intra", 0), ("intra", 1)])
     for i in range(2):
         add(("intra", i), 0.9, mixes + convs)
     for rel in RELS:
-        add(("mul", 1, rel, "A"), 0.5, [("conv", rel)], [(1, rel, "A")])
-        add(("mul", 1, rel, "B"), 0.7, [("conv", rel)], [(1, rel, "B")])
+        add(("mul", 1, rel, "A"), 0.35, [("conv", rel)], [(1, rel, "A")])
+        add(("mul", 1, rel, "B"), 0.32, [("conv", rel)], [(1, rel, "B")])
     return p
 
 
@@ -496,22 +496,22 @@
     def piece_mul(h, rel, route):
         i = RELS.index(rel)
         held, k0, kn = (wa, 0, KA) if route == "A" else (wb, KA, KB)
-        lhs = held[h, yy(rel)].reshape(NZ * 40, kn)
+        whole = [held[h, yy(rel), q] for q in range(NZ)]
+        lhs = [
+            jnp.concatenate([v[20 * e : 20 * e + 20, :] for v in whole], axis=0) for e in (0, 1)
+        ]
         for cols in (slice(0, 256), slice(256, 512), slice(512, 640))[: 3 - h]:
             n = slice(128 * h + cols.start, 128 * h + cols.stop)
-            for e in (0, 1):
-                v = dot(lhs, nt[1280 * e + k0 : 1280 * e + k0 + kn, n])
-                if (h, rel) in begun:
-                    acc[i, e, :, cols] += v
-                else:
-                    acc[i, e, :, cols] = v
+            v = dot(lhs[0], nt[k0 : k0 + kn, n]) + dot(lhs[1], nt[1280 + k0 : 1280 + k0 + kn, n])
+            if (h, rel) in begun:
+                acc[i, :, cols] += v
+            else:
+                acc[i, :, cols] = v
         begun.add((h, rel))
 
     def unfold(rel, into, width):
         i, r = RELS.index(rel), yy(rel)
-        for e in range(NZ):
-            v = acc[i, 0, 40 * e : 40 * e + 20, :width] + acc[i, 1, 40 * e + 20 : 40 * e + 40, :width]
-            into[r, 20 * e : 20 * e + 20, :] = v.astype(BF).astype(F32)
+        into[r] = acc[i, :, :width].astype(BF).astype(F32)
 
     def piece_conv(r):
         def step(i, carry):
@@ -805,7 +805,7 @@
         V((HEADS, 2, SPAN, SPAN), BF),
         V((128, TOK), F32),
         V((TOK, 128), F32),
-        V((4, 2, 320, 640), F32),
+        V((4, 160, 640), F32),
         V((160, TOK), F32),
         V((NY, 160, 640), F32),
         V((NY, 160, TOK), F32),

time: 82 us -> 81.1 us (0.989)
  Pallas kernels: 80.2 us -> 79.3 us
    pallas_call x1, Pallas kernels: 80.2 us -> 79.3 us  [run(): pl.pallas_call(kernel, out_shape=jax.ShapeDtypeStruct((FEAT, TOK), BF), i...]
where the time goes in v5:
time: 81.1 us; the launch traced here: 81 us
  Pallas kernels  79.3 us (98%)
  local copies, waits for them, and re-layouts  1.72 us (2%)
    pallas_call x1, Pallas kernels, run(): pl.pallas_call(kernel, out_shape=jax.ShapeDtypeStruct((FEAT, TOK), BF), i...  79.3 us
    unnamed x1, local copies, waits for them, and re-layouts  1.72 us

profile of v5, /device:TPU:1, one launch (start us, length us, event | category | flops | bytes accessed | tf_op | source)
XLA Modules:
  0.0 81.0 jit_solution(10241309125910485498)
XLA Ops:
  0.0 79.3 %layer.1 = bf16[320,512]{1,0:T(8,128)(2,1)} custom-call(bf16[512,2560]{1,0:T(8,128)(2,1)} %tok_in.1, f32[2560]{0:T(1024)} %gain_in.1, bf16[20,2,2560]{2,1,0:T(2,128)(2,1)} %bitcast.6, bf16[2560,2,128]{2,1,0:T(2,128)(2,1)} %sw_in.1, bf16[10,2560]{1,0:T(8,128)(2,1)} %bitcast.7, f32[10]{0:T(128)} %bias_in.1, f32[10]{0:T(128)} %rate_in.1, f32[10]{0:T(128)} %skip_in.1, ...), custom_call_target="tpu_custom_call" | custom-call | tf_op jit(solution)/shard_map/layer/pallas_call | solution.py:841
  79.3 1.7 %copy.14 = bf16[512,320]{0,1:T(8,128)(2,1)} copy(bf16[512,320]{0,1:T(8,128)(2,1)} %bitcast.5) | data formatting | bytes 655360

commit v6 on v5

--- a/solution.py
+++ b/solution.py
@@ -210,7 +210,7 @@
     out,
     gain, own_in, st, bias, rate, skip, cw_in, cwst, og_in,
     tok, own_a, own_b, own_f, sw, swd, cwin, og, wa, wb, nrm, nt, spf, cb, ct, dec, cum, ecum, tailw, d01, scores, mix, term, colt,
-    acc, joined, inn, gat, vt, vw, u, yv, cs, cr, co, ci, tt, rowd, prefix,
+    acc, joined, inn, gat, vt, vw, u, yv, cs, cr, co, ci, tt, rowd, lead, prefix,
     sbf, scb, wr, relay, sq, rs_out, rs_in1, rs2_out, rs2_in, keep, own_p,
     halo, send, recv, xsend, xrecv, lsem,
 ):
@@ -464,8 +464,9 @@
     def piece_dec_recv():
         for q in dec_copies:
             q.wait_recv()
-        prod = dec[0]
-        for k in range(1, NZ):
+        prod = jnp.ones((HEADS, 1, 128), F32)
+        for k in range(NZ):
+            lead[k] = prod
             prod = prod * dec[k]
         rowd[4] = prod
         rowd[y] = prod
@@ -573,12 +574,11 @@
         r = jnp.zeros((HEADS, 8, 128), F32)
         for k in range(NY - 1):
             r = jnp.where(y > k, r * rowd[k] + tt[k].astype(F32), r)
-        for k in range(NZ):
-            co[k] = (prefix[k] + r).astype(BF)
-            r = r * dec[k]
-        ci[z] = co[z]
         for k in FAR_FIRST:
+            co[zz(k)] = (prefix[zz(k)] + r * lead[zz(k)]).astype(BF)
             carry3.append(extra(co.at[zz(k)], ci.at[z], dev(dz=k), 20 + k))
+
+        ci[z] = (prefix[z] + r * lead[z]).astype(BF)
 
     def piece_carry4():
         for q in carry3:
@@ -819,6 +819,7 @@
         V((NZ, HEADS, 8, 128), BF),
         V((5, HEADS, 8, 128), BF),
         V((5, HEADS, 1, 128), F32),
+        V((NZ, HEADS, 1, 128), F32),
         V((NZ, HEADS, 8, 128), F32),
         V((2, CH, 128), BF),
         V((2, CH, TOK), BF),

time: 81.1 us -> 81.1 us (level)
  no operation moved by 1% of the time
where the time goes in v6:
time: 81.1 us; the launch traced here: 81 us
  Pallas kernels  79.3 us (98%)
  local copies, waits for them, and re-layouts  1.72 us (2%)
    pallas_call x1, Pallas kernels, run(): pl.pallas_call(kernel, out_shape=jax.ShapeDtypeStruct((FEAT, TOK), BF), i...  79.3 us
    unnamed x1, local copies, waits for them, and re-layouts  1.72 us

profile of v6, /device:TPU:1, one launch (start us, length us, event | category | flops | bytes accessed | tf_op | source)
XLA Modules:
  0.0 81.0 jit_solution(5039989885010175961)
XLA Ops:
  0.0 79.3 %layer.1 = bf16[320,512]{1,0:T(8,128)(2,1)} custom-call(bf16[512,2560]{1,0:T(8,128)(2,1)} %tok_in.1, f32[2560]{0:T(1024)} %gain_in.1, bf16[20,2,2560]{2,1,0:T(2,128)(2,1)} %bitcast.6, bf16[2560,2,128]{2,1,0:T(2,128)(2,1)} %sw_in.1, bf16[10,2560]{1,0:T(8,128)(2,1)} %bitcast.7, f32[10]{0:T(128)} %bias_in.1, f32[10]{0:T(128)} %rate_in.1, f32[10]{0:T(128)} %skip_in.1, ...), custom_call_target="tpu_custom_call" | custom-call | tf_op jit(solution)/shard_map/layer/pallas_call | solution.py:842
  79.3 1.7 %copy.14 = bf16[512,320]{0,1:T(8,128)(2,1)} copy(bf16[512,320]{0,1:T(8,128)(2,1)} %bitcast.5) | data formatting | bytes 655360
